TPU v7x, 32 devices: a whole 2x2x4 slice. The times are simulated.
32 devices in a mesh: dp: 2 (over x), ty: 4 (over z), tx: 4 (over y, core).
Axes of the slice: x: 2, y: 2, z: 4, core: 2. Of those that a mesh axis runs over, the one named last changes fastest.
Arguments:
- x_in: bfloat16 [8, 1024, 2048], P(('dp', 'ty'), None, 'tx'), parts along dimension 0
- w_q: bfloat16 [2048, 2048], P('tx', 'ty')
- w_k: bfloat16 [2048, 2048], P('tx', 'ty')
- w_v: bfloat16 [2048, 2048], P('tx', 'ty')
- w_o: bfloat16 [2048, 2048], P('ty', 'tx')
- w_gate: bfloat16 [2048, 8192], P('tx', 'ty')
- w_up: bfloat16 [2048, 8192], P('tx', 'ty')
- w_down: bfloat16 [8192, 2048], P('ty', 'tx')
Outputs:
- output: bfloat16 [8, 1024, 2048], P(('dp', 'ty'), None, 'tx'), parts along dimension 0
There are 2 independent parts. A program takes and returns all parts, laid end to end along the dimension named above; an argument that names none is the same for every part.
All inputs are finite; a program needn't handle non-finite values.
Results may differ from a plain program's by a relative error of at most 0.02.
Values are sent between devices in bfloat16 or wider.
A program may use at most 1 GiB of HBM per device.

v0:
```python
import jax
import jax.numpy as jnp
from jax import lax
from jax.sharding import PartitionSpec as P, NamedSharding

HEAD_DIM = 128
EPS = 1e-5
THETA = 10000.0


def rotary(heads_bf):
    seq_len = heads_bf.shape[1]
    half_dim = HEAD_DIM // 2
    inv_freq = THETA ** (-2.0 * jnp.arange(half_dim, dtype=jnp.float32) / HEAD_DIM)
    angles = jnp.arange(seq_len, dtype=jnp.float32)[:, None] * inv_freq[None, :]
    cos_t = jnp.cos(angles)[:, None, :]
    sin_t = jnp.sin(angles)[:, None, :]
    values = heads_bf.astype(jnp.float32)
    lower_half = values[..., :half_dim]
    upper_half = values[..., half_dim:]
    return jnp.concatenate([lower_half * cos_t - upper_half * sin_t, upper_half * cos_t + lower_half * sin_t], axis=-1).astype(jnp.bfloat16)


def causal_attention(q_heads, k_heads, v_heads):
    seq_len = q_heads.shape[1]
    q_block = min(seq_len, 128)
    key_pos = jnp.arange(seq_len)
    scale_qk = HEAD_DIM ** -0.5

    def one_block(block_idx, out_acc):
        q_start = block_idx * q_block
        q_blk = lax.dynamic_slice_in_dim(q_heads, q_start, q_block, axis=1)
        scores = jnp.einsum("nqhd,nkhd->nhqk", q_blk, k_heads, preferred_element_type=jnp.float32) * scale_qk
        q_pos = q_start + jnp.arange(q_block)
        allowed = q_pos[:, None] >= key_pos[None, :]
        scores = jnp.where(allowed, scores, -1e30)
        prob_blk = jax.nn.softmax(scores, axis=-1).astype(jnp.bfloat16)
        blk_out = jnp.einsum("nhqk,nkhd->nqhd", prob_blk, v_heads, preferred_element_type=jnp.float32).astype(jnp.bfloat16)
        return lax.dynamic_update_slice_in_dim(out_acc, blk_out, q_start, axis=1)

    return lax.fori_loop(0, seq_len // q_block, one_block, jnp.zeros_like(q_heads))


def norm_sharded(values_bf, full_width):
    values = values_bf.astype(jnp.float32)
    moments = jnp.stack([jnp.sum(values, axis=-1), jnp.sum(values * values, axis=-1)], axis=-1)
    moments = lax.psum(moments, "tx")
    mean_val = moments[..., 0:1] / full_width
    var_val = moments[..., 1:2] / full_width - mean_val * mean_val
    return ((values - mean_val) * lax.rsqrt(var_val + EPS)).astype(jnp.bfloat16)


def project(rows_bf, weight):
    return jnp.einsum("...c,ch->...h", rows_bf, weight, preferred_element_type=jnp.float32).astype(jnp.bfloat16)


def solution(mesh):
    tx_count = mesh.shape["tx"]
    act_spec = P(("dp", "ty"), None, "tx")
    col_spec = P("tx", "ty")
    row_spec = P("ty", "tx")

    def layer_fn(x_blk, w_q, w_k, w_v, w_o, w_gate, w_up, w_down):
        full_width = x_blk.shape[-1] * tx_count
        normed_all = lax.all_gather(norm_sharded(x_blk, full_width), "ty", axis=0, tiled=True)
        q_sum, k_sum, v_sum = lax.psum((project(normed_all, w_q), project(normed_all, w_k), project(normed_all, w_v)), "tx")
        n_seqs, seq_len, local_cols = q_sum.shape
        head_shape = (n_seqs, seq_len, local_cols // HEAD_DIM, HEAD_DIM)
        attn_heads = causal_attention(rotary(q_sum.reshape(head_shape)), rotary(k_sum.reshape(head_shape)), v_sum.reshape(head_shape))
        attn_out = lax.psum_scatter(project(attn_heads.reshape(q_sum.shape), w_o), "ty", scatter_dimension=0, tiled=True)
        resid_h = (x_blk.astype(jnp.float32) + attn_out.astype(jnp.float32)).astype(jnp.bfloat16)
        normed_mlp = lax.all_gather(norm_sharded(resid_h, full_width), "ty", axis=0, tiled=True)
        gate_sum, up_sum = lax.psum((project(normed_mlp, w_gate), project(normed_mlp, w_up)), "tx")
        act_val = (jax.nn.silu(gate_sum.astype(jnp.float32)) * up_sum.astype(jnp.float32)).astype(jnp.bfloat16)
        mlp_out = lax.psum_scatter(project(act_val, w_down), "ty", scatter_dimension=0, tiled=True)
        return (resid_h.astype(jnp.float32) + mlp_out.astype(jnp.float32)).astype(jnp.bfloat16)

    return jax.shard_map(layer_fn, mesh=mesh, in_specs=(act_spec, col_spec, col_spec, col_spec, row_spec, col_spec, col_spec, row_spec), out_specs=act_spec, check_vma=False)
```

profile of v0, /device:TPU:1, one launch (start us, length us, event | category | flops | bytes accessed | tf_op | source)
XLA Modules:
  0.0 1372.8 jit_solution(4732155398475219565)
XLA Ops:
  8.3 6.5 psum.49
  14.8 2.5 fusion.27
  17.4 81.8 %all-gather.3.cloned.1.call-done = bf16[4,1024,512]{2,1,0:T(8,128)(2,1)} async-done(((bf16[1,1024,512]{2,1,0:T(8,128)(2,1)}), bf16[4,1024,512]{2,1,0:T(8,128)(2,1)}) %all-gather.3.cloned.1.call-update) | async-done | bytes 4194320 | tf_op jit(solution)/shard_map/all_gather | solution.py:65
  99.3 6.5 convolution_convert_fusion.3
  105.8 6.3 copy.28
  112.1 6.5 convolution_convert_fusion.5
  118.6 6.3 copy.24
  124.9 6.5 convolution_convert_fusion.4
  131.4 6.2 copy.26
  137.9 2.7 fusion.41
  140.6 216.1 %all-reduce.7.cloned.1.call-done = (bf16[4,1024,4,128]{3,1,2,0:T(8,128)(2,1)}, bf16[4,1024,4,128]{3,1,2,0:T(8,128)(2,1)}, bf16[4,1024,4,128]{3,1,2,0:T(8,128)(2,1)}) async-done(((bf16[4,1024,4,128]{3,1,2,0:T(8,128)(2,1)}, bf16[4,1024,4,128]{3,1,2,0:T(8,128)(2,1)}, bf16[4,1024,4,128]{3,1,2,0:T(8,128)(2,1)}), (bf16[4,1024,4,128]{3,1,2,0:T(8,128)(2,1)}, bf16[4,1024,4,128]{3,1,2,0:T(8,128)(2,1)}, ...) | async-done | bytes 12582928 | tf_op jit(solution)/shard_map/psum | solution.py:66
  356.7 3.2 convert_element_type.91
  361.0 9.5 subtract_convert_fusion
  370.5 10.2 pad_maximum_fusion
  383.1 126.0 %while.14 = (s32[]{:T(128)}, bf16[4,1024,4,128]{1,3,2,0:T(8,128)(2,1)}, bf16[4,1024,4,128]{3,1,2,0:T(8,128)(2,1)}, bf16[4,1024,4,128]{3,1,2,0:T(8,128)(2,1)}, bf...) while((s32[]{:T(128)}, ...), condition=%wide.region_9.10_spmd.clone, body=%wide.region_6.9_spmd.clone.sunk | while | flops 1090913408 | bytes 62145712 | solution.py:41
  383.3 3.6 fusion.64
  386.9 5.8 fusion.65
  392.7 5.0 fusion.66
  399.0 3.6 fusion.64
  402.6 5.8 fusion.65
  408.4 5.0 fusion.66
  414.7 3.6 fusion.64
  418.4 5.8 fusion.65
  424.2 5.0 fusion.66
  430.5 3.6 fusion.64
  434.1 5.8 fusion.65
  439.9 4.9 fusion.66
  446.2 3.6 fusion.64
  449.8 5.8 fusion.65
  455.6 4.9 fusion.66
  461.9 3.6 fusion.64
  465.5 5.8 fusion.65
  471.3 4.9 fusion.66
  477.6 3.6 fusion.64
  481.2 5.8 fusion.65
  487.0 5.0 fusion.66
  493.3 3.6 fusion.64
  497.0 5.8 fusion.65
  502.8 5.0 fusion.66
  509.1 6.6 convolution_convert_fusion.2
  515.8 76.5 %reduce-scatter.3.cloned.1.call-done = bf16[1,1024,512]{2,1,0:T(8,128)(2,1)} async-done(((bf16[4,1024,512]{2,1,0:T(8,128)(2,1)}), bf16[1,1024,512]{2,1,0:T(8,128)(2,1)}) %reduce-scatter.3.cloned.1.call-update) | async-done | bytes 1048592 | tf_op jit(solution)/shard_map/reduce_scatter | solution.py:70
  594.4 6.7 psum.53
  602.5 80.9 %all-gather.5.cloned.1.call-done = bf16[4,1024,512]{2,1,0:T(8,128)(2,1)} async-done(((bf16[1,1024,512]{2,1,0:T(8,128)(2,1)}), bf16[4,1024,512]{2,1,0:T(8,128)(2,1)}) %all-gather.5.cloned.1.call-update) | async-done | bytes 4194320 | tf_op jit(solution)/shard_map/all_gather | solution.py:72
  683.5 14.7 %convolution_convert_fusion = bf16[4,1024,2048]{2,1,0:T(8,128)(2,1)} fusion(bf16[4,1024,512]{2,1,0:T(8,128)(2,1)} %all-gather.5.cloned.1.call-done, bf16[512,2048]{1,0:T(8,128)(2,1)S(1)} %copy-done), kind=kOutput, calls=%fused_computation.28 | convolution fusion | flops 8598323200 | bytes 23068672 | tf_op jit(solution)/shard_map/...c,ch->...h/dot_general | solution.py:54
  698.2 11.7 convolution_convert_fusion.1
  710.0 556.6 %all-reduce.5.cloned.1.call-done = (bf16[4,1024,2048]{2,1,0:T(8,128)(2,1)}, bf16[4,1024,2048]{2,1,0:T(8,128)(2,1)}) async-done(((bf16[4,1024,2048]{2,1,0:T(8,128)(2,1)}, bf16[4,1024,2048]{2,1,0:T(8,128)(2,1)}), (bf16[4,1024,2048]{2,1,0:T(8,128)(2,1)}, bf16[4,1024,2048]{2,1,0:T(8,128)(2,1)})) %all-reduce.5.cloned.1.call-update) | async-done | bytes 33554448 | tf_op jit(solution)/shard_map/psum | solution.py:73
  1266.6 20.1 %fusion.22 = bf16[4,1024,512]{2,1,0:T(8,128)(2,1)} fusion(bf16[4,1024,2048]{2,1,0:T(8,128)(2,1)} %get-tuple-element.141, bf16[4,1024,2048]{2,1,0:T(8,128)(2,1)} %get-tuple-element.142, bf16[2048,512]{1,0:T(8,128)(2,1)} %param.17), kind=kOutput, calls=%fused_computation.48 | convolution fusion | flops 8659140608 | bytes 39845888 | tf_op jit(solution)/shard_map/...c,ch->...h/dot_general | solution.py:54
  1286.8 76.2 %reduce-scatter.5.cloned.1.call-done = bf16[1,1024,512]{2,1,0:T(8,128)(2,1)} async-done(((bf16[4,1024,512]{2,1,0:T(8,128)(2,1)}), bf16[1,1024,512]{2,1,0:T(8,128)(2,1)}) %reduce-scatter.5.cloned.1.call-update) | async-done | bytes 1048592 | tf_op jit(solution)/shard_map/reduce_scatter | solution.py:75
  (85 shorter events, 22.4 us)
Async XLA Ops:
  6.5 677.0 %copy-start = (bf16[512,2048]{1,0:T(8,128)(2,1)S(1)}, bf16[512,2048]{1,0:T(8,128)(2,1)}, u32[]{:S(2)}) copy-start(bf16[512,2048]{1,0:T(8,128)(2,1)} %param.16) | copy-start | bytes 6291460
  6.5 92.7 %copy-start.5 = (bf16[512,512]{1,0:T(8,128)(2,1)S(1)}, bf16[512,512]{1,0:T(8,128)(2,1)}, u32[]{:S(2)}) copy-start(bf16[512,512]{1,0:T(8,128)(2,1)} %param.13) | copy-start | bytes 1572868
  6.5 92.7 %all-gather.3.cloned.1.call-start = ((), (), s32[]{:S(2)}) async-start(), calls=%async_computation.2 | async-start | bytes 5242880 | tf_op jit(solution)/shard_map/all_gather | solution.py:65
  17.4 339.3 %all-reduce.7.cloned.1.call-start = ((), (), s32[]{:S(2)}) async-start(), calls=%async_computation.7 | async-start | bytes 25165824 | tf_op jit(solution)/shard_map/psum | solution.py:66
  105.8 6.3 copy-start.6
  118.6 6.3 copy-start.7
  137.7 454.7 %reduce-scatter.3.cloned.1.call-start = ((), (), s32[]{:S(2)}) async-start(), calls=%async_computation.3 | async-start | bytes 5242880 | tf_op jit(solution)/shard_map/reduce_scatter | solution.py:70
  356.7 3.4 copy-start.1
  386.9 5.8 copy-start.2
  402.6 5.8 copy-start.2
  418.4 5.8 copy-start.2
  434.1 5.8 copy-start.2
  449.8 5.8 copy-start.2
  465.5 5.8 copy-start.2
  481.2 5.8 copy-start.2
  497.0 5.8 copy-start.2
  515.8 167.7 %all-gather.5.cloned.1.call-start = ((), (), s32[]{:S(2)}) async-start(), calls=%async_computation.4 | async-start | bytes 5242880 | tf_op jit(solution)/shard_map/all_gather | solution.py:72
  602.5 664.1 %all-reduce.5.cloned.1.call-start = ((), (), s32[]{:S(2)}) async-start(), calls=%async_computation.6 | async-start | bytes 67108864 | tf_op jit(solution)/shard_map/psum | solution.py:73
  683.5 14.7 %copy-start.3 = (bf16[4,1024,512]{2,1,0:T(8,128)(2,1)S(1)}, bf16[4,1024,512]{2,1,0:T(8,128)(2,1)}, u32[]{:S(2)}) copy-start(bf16[4,1024,512]{2,1,0:T(8,128)(2,1)} %all-gather.5.cloned.1.call-done) | copy-start | bytes 12582916
  683.5 14.7 %copy-start.4 = (bf16[512,2048]{1,0:T(8,128)(2,1)S(1)}, bf16[512,2048]{1,0:T(8,128)(2,1)}, u32[]{:S(2)}) copy-start(bf16[512,2048]{1,0:T(8,128)(2,1)} %param.15) | copy-start | bytes 6291460
  710.0 653.0 %reduce-scatter.5.cloned.1.call-start = ((), (), s32[]{:S(2)}) async-start(), calls=%async_computation.5 | async-start | bytes 5242880 | tf_op jit(solution)/shard_map/reduce_scatter | solution.py:75
Sparse Core Ops, SparseCore 0:
  17.5 81.7 all-gather.2
  137.8 218.8 all-reduce.6
  515.9 76.3 reduce-scatter.2
  602.6 80.8 all-gather.4
  710.1 556.5 all-reduce.4
  1286.9 76.0 reduce-scatter.4
where the time goes:
time: 1380 us; the launch traced here: 1370 us
  waiting for transfers between devices  1090 us (79%)
  matrix products  141 us (10%)
  other arithmetic  84 us (6%)
  local copies, waits for them, and re-layouts  31 us (2%)
  between operations  14 us (1%)
    psum x1, waiting for transfers between devices, layer_fn(): lax.psum((project(normed_mlp, w_gate), project(normed_mlp, w_up)), 'tx')  557 us
    psum x1, waiting for transfers between devices, layer_fn(): lax.psum((project(normed_all, w_q), project(normed_all, w_k), project(nor...  216 us
    all_gather x1, waiting for transfers between devices, layer_fn(): lax.all_gather(norm_sharded(x_blk, full_width), 'ty', axis=0, tiled=True)  81.8 us
    all_gather x1, waiting for transfers between devices, layer_fn(): lax.all_gather(norm_sharded(resid_h, full_width), 'ty', axis=0, tiled=True)  80.9 us
    reduce_scatter x1, waiting for transfers between devices, layer_fn(): lax.psum_scatter(project(attn_heads.reshape(q_sum.shape), w_o), 'ty', sca...  76.5 us
    reduce_scatter x1, waiting for transfers between devices, layer_fn(): lax.psum_scatter(project(act_val, w_down), 'ty', scatter_dimension=0, til...  76.2 us
    dot_general x7, matrix products, project(): jnp.einsum('...c,ch->...h', rows_bf, weight, preferred_element_type=jnp.f...  72.7 us
    sub x8, other arithmetic, one_block(): prob_blk = jax.nn.softmax(scores, axis=-1).astype(jnp.bfloat16)  46.3 us
  transfers between devices with their start and end apart: 6, of which 6 were waited for; matrix products, arithmetic and copies ran while one was open for 0% of the time, Pallas kernels for 0%

commit v1 on v0

v1 whole, which is shorter than its diff:
```python
import functools

import jax
import jax.numpy as jnp
from jax import lax
from jax.experimental import pallas as pl
from jax.experimental.pallas import tpu as pltpu
from jax.sharding import PartitionSpec as P

HEAD_DIM = 128
EPS = 1e-5
THETA = 10000.0
Q_BLOCK = 256
N_TILE = 256
CHUNKS = 4
N_TX = 4
N_TY = 4

f32, bf16 = jnp.float32, jnp.bfloat16


def rotary_tables(seq_len):
    half_dim = HEAD_DIM // 2
    inv_freq = THETA ** (-2.0 * jnp.arange(half_dim, dtype=jnp.float32) / HEAD_DIM)
    angles = jnp.arange(seq_len, dtype=jnp.float32)[:, None] * inv_freq[None, :]
    cos_t, sin_t = jnp.cos(angles), jnp.sin(angles)
    return jnp.concatenate([cos_t, cos_t], axis=1), jnp.concatenate([-sin_t, sin_t], axis=1)


def layer_norm(values):
    mean_val = jnp.mean(values, axis=-1, keepdims=True)
    var_val = jnp.mean(values * values, axis=-1, keepdims=True) - mean_val * mean_val
    return ((values - mean_val) * lax.rsqrt(var_val + EPS)).astype(bf16)


def layer_kernel(x_ref, wq_ref, wk_ref, wv_ref, wo_ref, wg_ref, wu_ref, wd_ref, cos_ref, sin_ref, y_ref,
                 x_all, w_all, wo_all, qkv_v, o_all, h_v, gate_v, up_v, down_v, h_rows, n_buf, act_v, work, landing, landing2, y_in,
                 loc_sem, x_send, x_recv, q_send, q_recv, z_send, z_recv, zx_send, zx_recv, p_send, p_recv, px_send, px_recv,
                 og_send, og_recv, m1_send, m1_recv, my_send, my_recv, mx_send, mx_recv, mf_send, mf_recv,
                 a_send, a_recv, g_send, g_recv, s_send, lo_recv, hi_recv, c_send, c_recv):
    d, z, i = lax.axis_index("dp"), lax.axis_index("ty"), lax.axis_index("tx")
    yy, core = i // 2, i % 2
    n_tx, n_ty, chunks = N_TX, N_TY, CHUNKS
    seq_len, width = x_ref.shape
    full, ff = n_tx * width, gate_v.shape[1]
    quarter = seq_len // n_tx
    ch = quarter // chunks
    half_w = width // 2
    last = n_ty - 1
    MESH = pl.DeviceIdType.MESH

    def tx_to(k):
        return {"tx": i ^ k}

    def remote(src, dst, send, recv, where):
        return pltpu.make_async_remote_copy(src_ref=src, dst_ref=dst, send_sem=send, recv_sem=recv, device_id=where, device_id_type=MESH)

    def aligned(v, m):
        return pl.multiple_of(v, m)

    x_half = seq_len // 2

    def x_copy(c, k):
        rows = pl.ds(c * x_half, x_half)
        if k == 3:
            return remote(x_all.at[i ^ 2, rows], x_all.at[i ^ 2, rows], x_send.at[c, 3], x_recv.at[c, 3], tx_to(1))
        return remote(x_ref.at[rows], x_all.at[i, rows], x_send.at[c, k], x_recv.at[c, k], tx_to(k))

    mats = (wq_ref, wk_ref, wv_ref)

    def q_copy(k, m, h):
        src = mats[m].at[pl.ds(aligned(h * half_w, half_w), half_w), pl.ds(aligned((i ^ k) * HEAD_DIM, HEAD_DIM), HEAD_DIM)]
        dst = w_all.at[z, h, yy, pl.ds(aligned(core * half_w, half_w), half_w), pl.ds(m * HEAD_DIM, HEAD_DIM)]
        if k == 0:
            return pltpu.make_async_copy(src, dst, q_recv.at[0, m, h])
        return remote(src, dst, q_send.at[k, m, h], q_recv.at[k, m, h], tx_to(k))

    def chip_of(g):
        return yy if g == 0 else 1 - yy

    def z_copy(src, g, step):
        block = w_all.at[src, d, chip_of(g)]
        return remote(block, block, z_send.at[src, g, (step + 1) // 2], z_recv.at[src, g], {"ty": z + step})

    def zx_copy(src, g):
        block = w_all.at[src, d, chip_of(g)]
        return remote(block, block, zx_send.at[src, g], zx_recv.at[src, g], {"dp": 1 - d})

    def p_rows():
        return pl.ds(aligned(d * half_w, half_w), half_w)

    def p_copy(src, step):
        block = wo_all.at[src, p_rows()]
        return remote(block, block, p_send.at[src, (step + 1) // 2], p_recv.at[src], {"ty": z + step})

    def px_copy(src):
        block = wo_all.at[src, p_rows()]
        return remote(block, block, px_send.at[src], px_recv.at[src], {"dp": 1 - d})

    def og_copy(src, k):
        head = (i ^ 2) if k == 3 else i
        block = o_all.at[:, pl.ds(aligned(src * width + head * HEAD_DIM, HEAD_DIM), HEAD_DIM)]
        return remote(block, block, og_send.at[src, k], og_recv.at[src, k], tx_to(1 if k == 3 else k))

    own_w, full_w = (wg_ref, wu_ref, wd_ref), (gate_v, up_v, down_v)
    q_rows = (half_w // 2, half_w // 2, ff // 4)

    def m_span(a, h, q):
        return pl.ds(aligned((h * 2 + q) * q_rows[a], q_rows[a]), q_rows[a])

    def m_slot(a, k, h, q):
        if a == 2:
            return down_v.at[m_span(a, h, q), pl.ds(k * width, width)]
        return full_w[a].at[pl.ds(aligned(k * width + (h * 2 + q) * q_rows[a], q_rows[a]), q_rows[a])]

    def m_block(a, k):
        if a == 2:
            return down_v.at[:, pl.ds(k * width, width)]
        return full_w[a].at[pl.ds(k * width, width)]

    def m_own(a):
        return pltpu.make_async_copy(own_w[a], m_block(a, 0), loc_sem.at[a])

    def m_near(a):
        return remote(own_w[a], m_block(a, 1), m1_send.at[a], m1_recv.at[a], tx_to(1))

    def m_far(a, q):
        return remote(own_w[a].at[m_span(a, d, q)], m_slot(a, 2, d, q), my_send.at[a, q], my_recv.at[a, q], tx_to(2))

    def m_swap(a, q):
        return remote(m_slot(a, 2, d, q), m_slot(a, 2, d, q), mx_send.at[a, q], mx_recv.at[a, q], {"dp": 1 - d})

    def m_pass(a, q, h):
        return remote(m_slot(a, 2, h, q), m_slot(a, 3, h, q), mf_send.at[a, q, h], mf_recv.at[a, q, h], tx_to(1))

    PIECES = [(a, q) for a in range(3) for q in range(2)]

    def m_far_start(p):
        m_far(*PIECES[p]).start()

    def m_far_done(p):
        a, q = PIECES[p]
        m_far(a, q).wait_recv()
        m_swap(a, q).start()
        m_pass(a, q, d).start()

    def m_swap_done(p):
        a, q = PIECES[p]
        m_swap(a, q).wait_recv()
        m_pass(a, q, 1 - d).start()

    def m_ready(a):
        m_own(a).wait()
        m_near(a).wait_recv()
        for q in range(2):
            for h in range(2):
                m_pass(a, q, h).wait_recv()

    def slot(c, dst):
        return pl.ds(aligned((c * n_ty + dst) * ch, ch), ch)

    def own_rows(c):
        return pl.ds(aligned(i * quarter + c * ch, ch), ch)

    def spread(c, k):
        rows = pl.ds(aligned((i ^ k) * quarter + c * ch, ch), ch)
        return remote(h_v.at[rows], h_rows.at[c, :, pl.ds(k * width, width)], a_send.at[c, k], a_recv.at[c, k], tx_to(k))

    def gather(c, src, step):
        return remote(n_buf.at[c, src], n_buf.at[c, src], g_send.at[c, src, (step + 1) // 2], g_recv.at[c, src], {"ty": z + step})

    def reduce(c, dst, step, final):
        src = work.at[slot(c, dst)]
        if step == 1:
            return remote(src, landing.at[slot(c, dst)], s_send.at[c, dst], lo_recv.at[c, dst], {"ty": z + 1})
        if final:
            return remote(src, landing2.at[c], s_send.at[c, dst], hi_recv.at[c, 0], {"ty": z - 1})
        return remote(src, landing.at[slot(c, dst)], s_send.at[c, dst], lo_recv.at[c, dst], {"ty": z - 1})

    def collect(c, k):
        return remote(work.at[slot(c, z), pl.ds(k * width, width)], y_in.at[own_rows(c)], c_send.at[c, k], c_recv.at[c, k], tx_to(k))

    x_own = pltpu.make_async_copy(x_ref, x_all.at[i], loc_sem.at[3])
    wo_own = pltpu.make_async_copy(wo_ref, wo_all.at[z], loc_sem.at[4])
    for m in range(3):
        for h in range(2):
            q_copy(0, m, h).start()
    x_own.start()
    wo_own.start()

    barrier = pltpu.get_barrier_semaphore()
    for k in range(1, n_tx):
        pl.semaphore_signal(barrier, inc=1, device_id=tx_to(k), device_id_type=MESH)
    pl.semaphore_signal(barrier, inc=1, device_id={"dp": 1 - d}, device_id_type=MESH)

    @pl.when(z > 0)
    def _():
        pl.semaphore_signal(barrier, inc=1, device_id={"ty": z - 1}, device_id_type=MESH)

    @pl.when(z < last)
    def _():
        pl.semaphore_signal(barrier, inc=1, device_id={"ty": z + 1}, device_id_type=MESH)

    @pl.when((z > 0) & (z < last))
    def _():
        pl.semaphore_wait(barrier, n_tx + 2)

    @pl.when((z == 0) | (z == last))
    def _():
        pl.semaphore_wait(barrier, n_tx + 1)

    for m in range(3):
        q_copy(1, m, d).start()
    for k in (2, 3):
        for m in range(3):
            q_copy(k, m, d).start()
    for m in range(3):
        q_copy(1, m, 1 - d).start()
    for c in range(2):
        x_copy(c, 1).start()
    for c in range(2):
        x_copy(c, 2).start()
    for k in (2, 3):
        for m in range(3):
            q_copy(k, m, 1 - d).start()
    for a in range(3):
        m_own(a).start()

    def both_ways(make):
        @pl.when(z < last)
        def _():
            make(1).start()

        @pl.when(z > 0)
        def _():
            make(-1).start()

    def hop(make, swap, h):
        @pl.when(z >= h)
        def _():
            make(z - h, 1).wait_recv()

            @pl.when(z < last)
            def _():
                make(z - h, 1).start()

            if swap is not None:
                swap(z - h).start()

        @pl.when(z + h <= last)
        def _():
            make(z + h, -1).wait_recv()

            @pl.when(z > 0)
            def _():
                make(z + h, -1).start()

            if swap is not None:
                swap(z + h).start()

    def z_hop(g, h):
        hop(lambda src, step: z_copy(src, g, step), lambda src: zx_copy(src, g), h)

    def p_hop(h):
        hop(p_copy, px_copy, h)

    def norm_rows(c):
        block = 32

        def body(t, carry):
            rows = pl.ds(aligned(c * x_half + t * block, block), block)
            parts = [x_all[j, rows, :].astype(f32) for j in range(n_tx)]
            normed = layer_norm(jnp.concatenate(parts, axis=1))
            for j in range(n_tx):
                for h in range(2):
                    to = h * (full // 2) + j * half_w
                    work[rows, to:to + half_w] = normed[:, j * width + h * half_w:j * width + (h + 1) * half_w]
            return carry

        lax.fori_loop(0, x_half // block, body, 0)

    s = z // 2
    order = [z, 1 - z + 4 * s, 2 - s, 3 - 3 * s]

    def project_heads(src):
        tile = 256

        def body(t, carry):
            rows = pl.ds(aligned(t * tile, tile), tile)
            weight = w_all[src].reshape(full, 3 * HEAD_DIM)
            qkv_v[rows, :] = jnp.dot(work[rows, :], weight, preferred_element_type=f32).astype(bf16)
            return carry

        lax.fori_loop(0, seq_len // tile, body, 0)

    def rotate(values_bf, rows):
        values = values_bf.astype(f32)
        turned = values * cos_ref[rows, :] + pltpu.roll(values, HEAD_DIM // 2, 1) * sin_ref[rows, :]
        return turned.astype(bf16)

    def attend(src):
        cols = pl.ds(aligned(src * width + i * HEAD_DIM, HEAD_DIM), HEAD_DIM)
        k_rot = rotate(qkv_v[:, HEAD_DIM:2 * HEAD_DIM], slice(0, seq_len))
        v_all = qkv_v[:, 2 * HEAD_DIM:3 * HEAD_DIM]
        for blk in range(seq_len // Q_BLOCK):
            rows = slice(blk * Q_BLOCK, (blk + 1) * Q_BLOCK)
            keys = (blk + 1) * Q_BLOCK
            q_rot = rotate(qkv_v[rows, :HEAD_DIM], rows)
            scores = lax.dot_general(q_rot, k_rot[:keys], (((1,), (1,)), ((), ())), preferred_element_type=f32) * HEAD_DIM ** -0.5
            q_pos = blk * Q_BLOCK + lax.broadcasted_iota(jnp.int32, (Q_BLOCK, keys), 0)
            k_pos = lax.broadcasted_iota(jnp.int32, (Q_BLOCK, keys), 1)
            scores = jnp.where(q_pos >= k_pos, scores, -1e30)
            weights = jnp.exp(scores - jnp.max(scores, axis=-1, keepdims=True))
            probs = (weights * (1.0 / jnp.sum(weights, axis=-1, keepdims=True))).astype(bf16)
            o_all[rows, cols] = jnp.dot(probs, v_all[:keys], preferred_element_type=f32).astype(bf16)

    def og_start(r):
        og_copy(order[r], 2).start()
        og_copy(order[r], 1).start()

    def og_pass(r):
        og_copy(order[r], 2).wait_recv()
        og_copy(order[r], 3).start()

    def block_ready(r):
        for g in range(2):
            zx_copy(order[r], g).wait_recv()

    for m in range(3):
        for h in range(2):
            q_copy(0, m, h).wait()
        q_copy(1, m, d).wait_recv()
    both_ways(lambda step: z_copy(z, 0, step))
    for k in (2, 3):
        for m in range(3):
            q_copy(k, m, d).wait_recv()
    both_ways(lambda step: z_copy(z, 1, step))
    wo_own.wait()
    z_hop(0, 1)
    x_own.wait()
    for c in range(2):
        x_copy(c, 1).wait_recv()
    x_copy(0, 2).wait_recv()
    x_copy(0, 3).start()
    z_hop(1, 1)
    x_copy(0, 3).wait_recv()
    norm_rows(0)
    z_hop(0, 2)
    x_copy(1, 2).wait_recv()
    x_copy(1, 3).start()
    m_far_start(0)
    m_near(0).start()
    x_copy(1, 3).wait_recv()
    norm_rows(1)
    z_hop(1, 2)
    both_ways(lambda step: p_copy(z, step))
    for m in range(3):
        q_copy(1, m, 1 - d).wait_recv()
        for k in (2, 3):
            q_copy(k, m, 1 - d).wait_recv()
    project_heads(order[0])
    z_hop(0, 3)
    attend(order[0])
    og_start(0)
    m_far_start(1)
    m_near(1).start()
    z_hop(1, 3)
    block_ready(1)
    project_heads(order[1])
    m_far_done(0)
    p_hop(1)
    og_pass(0)
    attend(order[1])
    og_start(1)
    m_far_start(2)
    p_hop(2)
    block_ready(2)
    project_heads(order[2])
    m_far_done(1)
    p_hop(3)
    og_pass(1)
    attend(order[2])
    og_start(2)
    m_near(2).start()
    block_ready(3)
    project_heads(order[3])
    m_far_done(2)
    attend(order[3])
    og_start(3)
    m_far_start(3)
    m_far_start(4)
    og_pass(2)
    m_swap_done(0)
    og_pass(3)
    for r in range(1, n_ty):
        px_copy(order[r]).wait_recv()
    for r in range(n_ty):
        og_copy(order[r], 1).wait_recv()
        og_copy(order[r], 3).wait_recv()

    def out_project(t, carry):
        rows = pl.ds(aligned(t * 256, 256), 256)
        attn_out = jnp.dot(o_all[rows, :], wo_all[...].reshape(full, width), preferred_element_type=f32).astype(bf16)
        h_v[rows, :] = (x_all[i, rows, :].astype(f32) + attn_out.astype(f32)).astype(bf16)
        return carry

    lax.fori_loop(0, seq_len // 256, out_project, 0)

    for c in range(chunks):
        for k in (2, 3, 1):
            spread(c, k).start()
    m_far_start(5)
    m_swap_done(1)
    m_far_done(3)

    def norm_chunk(c):
        for k in range(1, n_tx):
            spread(c, k).wait_recv()
        h_rows[c, :, :width] = h_v[own_rows(c), :]
        block = min(ch, 32)
        for b in range(ch // block):
            rows = slice(b * block, (b + 1) * block)
            n_buf[c, z, rows, :] = layer_norm(h_rows[c, rows, :].astype(f32))

    def gather_own(c):
        both_ways(lambda step: gather(c, z, step))

    def gather_hop(c, h):
        hop(lambda src, step: gather(c, src, step), None, h)

    n_tiles, d_tiles = ff // N_TILE, full // N_TILE

    def gate_up(c, lo, hi):
        def body(t, carry):
            cols = pl.ds(aligned(t * N_TILE, N_TILE), N_TILE)
            rows = n_buf[c].reshape(n_ty * ch, full)
            gate_val = jnp.dot(rows, gate_v[:, cols], preferred_element_type=f32).astype(bf16).astype(f32)
            up_val = jnp.dot(rows, up_v[:, cols], preferred_element_type=f32).astype(bf16).astype(f32)
            act_v[:, cols] = (gate_val * jax.nn.sigmoid(gate_val) * up_val).astype(bf16)
            return carry

        lax.fori_loop(lo, hi, body, 0)

    def down(c, lo, hi):
        def body(t, carry):
            cols = pl.ds(aligned(t * N_TILE, N_TILE), N_TILE)
            work[pl.ds(c * n_ty * ch, n_ty * ch), cols] = jnp.dot(act_v[...], down_v[:, cols], preferred_element_type=f32).astype(bf16)
            return carry

        lax.fori_loop(lo, hi, body, 0)

    def compute(c, third):
        steps = n_tiles + d_tiles
        lo, hi = steps * third // 3, steps * (third + 1) // 3
        if lo < n_tiles:
            gate_up(c, lo, min(hi, n_tiles))
        if hi > n_tiles:
            if c == 0 and lo <= n_tiles:
                m_swap_done(4)
                m_swap_done(5)
                m_ready(2)
            down(c, max(lo, n_tiles) - n_tiles, hi - n_tiles)

    def add_into(c, dst):
        work[slot(c, dst), :] = (work[slot(c, dst), :].astype(f32) + landing[slot(c, dst), :].astype(f32)).astype(bf16)

    def reduce_hop(c, h):
        dist = n_ty - h

        @pl.when(z + dist <= last)
        def _():
            @pl.when(z > 0)
            def _():
                reduce(c, z + dist, 1, False).wait_recv()
                add_into(c, z + dist)

            reduce(c, z + dist, 1, False).start()

        @pl.when(z >= dist)
        def _():
            @pl.when(z < last)
            def _():
                reduce(c, z - dist, -1, False).wait_recv()
                add_into(c, z - dist)

            reduce(c, z - dist, -1, dist == 1).start()

    def reduce_end(c):
        @pl.when(z > 0)
        def _():
            reduce(c, z, 1, False).wait_recv()

        @pl.when(z < last)
        def _():
            reduce(c, z, -1, True).wait_recv()

        @pl.when(z == 0)
        def _():
            work[slot(c, z), :] = (work[slot(c, z), :].astype(f32) + landing2[c].astype(f32)).astype(bf16)

        @pl.when(z == last)
        def _():
            add_into(c, z)

        @pl.when((z > 0) & (z < last))
        def _():
            total = work[slot(c, z), :].astype(f32) + landing[slot(c, z), :].astype(f32) + landing2[c].astype(f32)
            work[slot(c, z), :] = total.astype(bf16)

        for k in (2, 3, 1):
            collect(c, k).start()
        y_in[own_rows(c), :] = work[slot(c, z), :width]

    norm_chunk(0)
    gather_own(0)
    for c in range(1, chunks):
        norm_chunk(c)
    m_swap_done(2)
    for t in range(chunks + 2):
        if 0 < t < chunks:
            gather_own(t)
        if t == 1:
            m_ready(0)
            m_swap_done(3)
            m_ready(1)
        for h in range(1, n_ty):
            if t >= 2:
                reduce_hop(t - 2, h)
            if 1 <= t <= chunks:
                compute(t - 1, h - 1)
            if t < chunks:
                gather_hop(t, h)
            if t == 0 and h == 1:
                m_far_done(4)
            if t == 0 and h == 3:
                m_far_done(5)
        if t >= 2:
            reduce_end(t - 2)

    for c in range(chunks):
        for k in range(1, n_tx):
            collect(c, k).wait_recv()

    def finish(t, carry):
        rows = pl.ds(aligned(t * 128, 128), 128)
        y_ref[rows, :] = (h_v[rows, :].astype(f32) + y_in[rows, :].astype(f32)).astype(bf16)
        return carry

    lax.fori_loop(0, seq_len // 128, finish, 0)

    for c in range(2):
        for k in range(1, n_tx):
            x_copy(c, k).wait_send()
    for k in range(1, n_tx):
        for m in range(3):
            q_copy(k, m, d).wait_send()
            q_copy(k, m, 1 - d).wait_send()
    for src in range(n_ty):
        for k in range(1, n_tx):
            og_copy(src, k).wait_send()
        for g in range(2):
            @pl.when((z >= src) & (z < last))
            def _():
                z_copy(src, g, 1).wait_send()

            @pl.when((z <= src) & (z > 0))
            def _():
                z_copy(src, g, -1).wait_send()

            @pl.when(z != src)
            def _():
                zx_copy(src, g).wait_send()

        @pl.when((z >= src) & (z < last))
        def _():
            p_copy(src, 1).wait_send()

        @pl.when((z <= src) & (z > 0))
        def _():
            p_copy(src, -1).wait_send()

        @pl.when(z != src)
        def _():
            px_copy(src).wait_send()
    for a in range(3):
        m_near(a).wait_send()
        for q in range(2):
            m_far(a, q).wait_send()
            m_swap(a, q).wait_send()
            for h in range(2):
                m_pass(a, q, h).wait_send()
    for c in range(chunks):
        for k in range(1, n_tx):
            spread(c, k).wait_send()
            collect(c, k).wait_send()
        for src in range(n_ty):
            @pl.when((z >= src) & (z < last))
            def _():
                gather(c, src, 1).wait_send()

            @pl.when((z <= src) & (z > 0))
            def _():
                gather(c, src, -1).wait_send()

            @pl.when(z < src)
            def _():
                reduce(c, src, 1, False).wait_send()

            @pl.when(z > src)
            def _():
                reduce(c, src, -1, False).wait_send()


def solution(mesh):
    act_spec = P(("dp", "ty"), None, "tx")
    col_spec = P("tx", "ty")
    row_spec = P("ty", "tx")
    dma = pltpu.SemaphoreType.DMA

    def layer_fn(x_blk, w_q, w_k, w_v, w_o, w_gate, w_up, w_down):
        seq_len, width = x_blk.shape[1:]
        full, ff = N_TX * width, w_gate.shape[1]
        ch = seq_len // N_TX // CHUNKS
        cos_t, sin_t = rotary_tables(seq_len)
        hbm = pl.BlockSpec(memory_space=pl.ANY)
        vmem = pl.BlockSpec(memory_space=pltpu.VMEM)
        out = pl.pallas_call(
            layer_kernel,
            out_shape=jax.ShapeDtypeStruct((seq_len, width), bf16),
            in_specs=[hbm] * 8 + [vmem] * 2,
            out_specs=vmem,
            scratch_shapes=[
                pltpu.VMEM((N_TX, seq_len, width), bf16),
                pltpu.VMEM((N_TY, 2, 2, width, 3 * HEAD_DIM), bf16),
                pltpu.VMEM((N_TY, width, width), bf16),
                pltpu.VMEM((seq_len, 3 * HEAD_DIM), bf16),
                pltpu.VMEM((seq_len, full), bf16),
                pltpu.VMEM((seq_len, width), bf16),
                pltpu.VMEM((full, ff), bf16),
                pltpu.VMEM((full, ff), bf16),
                pltpu.VMEM((ff, full), bf16),
                pltpu.VMEM((CHUNKS, ch, full), bf16),
                pltpu.VMEM((CHUNKS, N_TY, ch, full), bf16),
                pltpu.VMEM((N_TY * ch, ff), bf16),
                pltpu.VMEM((seq_len, full), bf16),
                pltpu.VMEM((seq_len, full), bf16),
                pltpu.VMEM((CHUNKS, ch, full), bf16),
                pltpu.VMEM((seq_len, width), bf16),
                dma((5,)),
                dma((2, 4)), dma((2, 4)),
                dma((4, 3, 2)), dma((4, 3, 2)),
                dma((N_TY, 2, 2)), dma((N_TY, 2)), dma((N_TY, 2)), dma((N_TY, 2)),
                dma((N_TY, 2)), dma((N_TY,)), dma((N_TY,)), dma((N_TY,)),
                dma((N_TY, 4)), dma((N_TY, 4)),
                dma((3,)), dma((3,)), dma((3, 2)), dma((3, 2)), dma((3, 2)), dma((3, 2)), dma((3, 2, 2)), dma((3, 2, 2)),
                dma((CHUNKS, N_TX)), dma((CHUNKS, N_TX)),
                dma((CHUNKS, N_TY, 2)), dma((CHUNKS, N_TY)),
                dma((CHUNKS, N_TY)), dma((CHUNKS, N_TY)), dma((CHUNKS, 1)),
                dma((CHUNKS, N_TX)), dma((CHUNKS, N_TX)),
            ],
            compiler_params=pltpu.CompilerParams(collective_id=1, has_side_effects=True, vmem_limit_bytes=67043328),
            cost_estimate=pl.CostEstimate(flops=8 * seq_len * full * ff, bytes_accessed=6 * full * ff, transcendentals=seq_len * ff),
            name="layer",
        )(x_blk[0], w_q, w_k, w_v, w_o, w_gate, w_up, w_down, cos_t, sin_t)
        return out[None]

    return jax.shard_map(layer_fn, mesh=mesh, in_specs=(act_spec, col_spec, col_spec, col_spec, row_spec, col_spec, col_spec, row_spec), out_specs=act_spec, check_vma=False)
```

time: 1380 us -> 276 us (0.20)
  waiting for transfers between devices: 1090 us -> 0 us
  Pallas kernels: 0 us -> 271 us
  matrix products: 141 us -> 0 us
  other arithmetic: 84 us -> 3.3 us
  local copies, waits for them, and re-layouts: 31 us -> 2.26 us
  between operations: 14 us -> 0.02 us
    psum x2 -> x0, waiting for transfers between devices: 773 us -> none  [the longest x1 557 us: layer_fn(): lax.psum((project(normed_mlp, w_gate), project(normed_mlp, w_up)), 'tx')]
    pallas_call x0 -> x1, Pallas kernels: none -> 271 us  [layer_fn(): pl.pallas_call(layer_kernel, out_shape=jax.ShapeDtypeStruct((seq_len, wid...]
    all_gather x2 -> x0, waiting for transfers between devices: 163 us -> none  [the longest x1 81.8 us: layer_fn(): lax.all_gather(norm_sharded(x_blk, full_width), 'ty', axis=0, tiled=True)]
    reduce_scatter x2 -> x0, waiting for transfers between devices: 153 us -> none  [the longest x1 76.5 us: layer_fn(): lax.psum_scatter(project(attn_heads.reshape(q_sum.shape), w_o), 'ty', sca...]
    dot_general x23 -> x0, matrix products: 141 us -> none  [the longest x7 72.7 us: project(): jnp.einsum('...c,ch->...h', rows_bf, weight, preferred_element_type=jnp.f...]
    sub x8 -> x0, other arithmetic: 46.3 us -> none  [one_block(): prob_blk = jax.nn.softmax(scores, axis=-1).astype(jnp.bfloat16)]
  transfers between devices with their start and end apart: 6 -> 0, of which waited for: 6 -> 0; matrix products, arithmetic and copies ran while one was open for 0% -> 0% of each run, Pallas kernels for 0% -> 0%
where the time goes in v1:
time: 276 us
  Pallas kernels  271 us (98%)
  other arithmetic  3.3 us (1%)
    pallas_call x1, Pallas kernels, layer_fn(): pl.pallas_call(layer_kernel, out_shape=jax.ShapeDtypeStruct((seq_len, wid...  271 us

profile of v1, /device:TPU:1, one launch (start us, length us, event | category | flops | bytes accessed | tf_op | source)
XLA Modules:
  0.0 276.2 jit_solution(2294526537405887675)
XLA Ops:
  0.0 2.0 fusion.2
  2.0 1.3 pad_maximum_fusion
  3.3 270.6 %layer.1 = bf16[1024,512]{1,0:T(8,128)(2,1)} custom-call(bf16[1024,512]{1,0:T(8,128)(2,1)} %bitcast.3, bf16[512,512]{1,0:T(8,128)(2,1)} %wq_ref.1, bf16[512,512]{1,0:T(8,128)(2,1)} %wk_ref.1, bf16[512,512]{1,0:T(8,128)(2,1)} %wv_ref.1, bf16[512,512]{1,0:T(8,128)(2,1)} %wo_ref.1, bf16[512,2048]{1,0:T(8,128)(2,1)} %wg_ref.1, bf16[512,2048]{1,0:T(8,128)(2,1)} %wu_ref.1, ...), custom_call_target="tpu_custom_call" | custom-call | flops 34359738368 | bytes 25165824 | tf_op jit(solution)/shard_map/layer/pallas_call | solution.py:627
  274.0 2.3 copy.10
  (1 shorter events, 0.0 us)

commit v2 on v1

--- a/solution.py
+++ b/solution.py
@@ -1,4 +1,4 @@
-import functools
+import math
 
 import jax
 import jax.numpy as jnp
@@ -15,16 +15,9 @@
 CHUNKS = 4
 N_TX = 4
 N_TY = 4
+N_PIECES = 4
 
 f32, bf16 = jnp.float32, jnp.bfloat16
-
-
-def rotary_tables(seq_len):
-    half_dim = HEAD_DIM // 2
-    inv_freq = THETA ** (-2.0 * jnp.arange(half_dim, dtype=jnp.float32) / HEAD_DIM)
-    angles = jnp.arange(seq_len, dtype=jnp.float32)[:, None] * inv_freq[None, :]
-    cos_t, sin_t = jnp.cos(angles), jnp.sin(angles)
-    return jnp.concatenate([cos_t, cos_t], axis=1), jnp.concatenate([-sin_t, sin_t], axis=1)
 
 
 def layer_norm(values):
@@ -33,8 +26,8 @@
     return ((values - mean_val) * lax.rsqrt(var_val + EPS)).astype(bf16)
 
 
-def layer_kernel(x_ref, wq_ref, wk_ref, wv_ref, wo_ref, wg_ref, wu_ref, wd_ref, cos_ref, sin_ref, y_ref,
-                 x_all, w_all, wo_all, qkv_v, o_all, h_v, gate_v, up_v, down_v, h_rows, n_buf, act_v, work, landing, landing2, y_in,
+def layer_kernel(x_ref, wq_ref, wk_ref, wv_ref, wo_ref, wg_ref, wu_ref, wd_ref, y_ref,
+                 x_all, w_all, wo_all, qkv_v, o_all, h_v, gate_v, up_v, down_v, h_rows, n_buf, work, landing, landing2, y_in, cos_ref, sin_ref,
                  loc_sem, x_send, x_recv, q_send, q_recv, z_send, z_recv, zx_send, zx_recv, p_send, p_recv, px_send, px_recv,
                  og_send, og_recv, m1_send, m1_recv, my_send, my_recv, mx_send, mx_recv, mf_send, mf_recv,
                  a_send, a_recv, g_send, g_recv, s_send, lo_recv, hi_recv, c_send, c_recv):
@@ -86,16 +79,14 @@
         block = w_all.at[src, d, chip_of(g)]
         return remote(block, block, zx_send.at[src, g], zx_recv.at[src, g], {"dp": 1 - d})
 
-    def p_rows():
-        return pl.ds(aligned(d * half_w, half_w), half_w)
+    def p_block(src):
+        return wo_all.at[src, pl.ds(aligned(d * half_w, half_w), half_w)]
 
     def p_copy(src, step):
-        block = wo_all.at[src, p_rows()]
-        return remote(block, block, p_send.at[src, (step + 1) // 2], p_recv.at[src], {"ty": z + step})
+        return remote(p_block(src), p_block(src), p_send.at[src, (step + 1) // 2], p_recv.at[src], {"ty": z + step})
 
     def px_copy(src):
-        block = wo_all.at[src, p_rows()]
-        return remote(block, block, px_send.at[src], px_recv.at[src], {"dp": 1 - d})
+        return remote(p_block(src), p_block(src), px_send.at[src], px_recv.at[src], {"dp": 1 - d})
 
     def og_copy(src, k):
         head = (i ^ 2) if k == 3 else i
@@ -103,15 +94,21 @@
         return remote(block, block, og_send.at[src, k], og_recv.at[src, k], tx_to(1 if k == 3 else k))
 
     own_w, full_w = (wg_ref, wu_ref, wd_ref), (gate_v, up_v, down_v)
-    q_rows = (half_w // 2, half_w // 2, ff // 4)
-
-    def m_span(a, h, q):
-        return pl.ds(aligned((h * 2 + q) * q_rows[a], q_rows[a]), q_rows[a])
+    q_span = ff // 2 // N_PIECES
+
+    def m_span(h, q):
+        return pl.ds(aligned((h * N_PIECES + q) * q_span, q_span), q_span)
 
     def m_slot(a, k, h, q):
+        side = pl.ds(k * width, width)
         if a == 2:
-            return down_v.at[m_span(a, h, q), pl.ds(k * width, width)]
-        return full_w[a].at[pl.ds(aligned(k * width + (h * 2 + q) * q_rows[a], q_rows[a]), q_rows[a])]
+            return down_v.at[m_span(h, q), side]
+        return full_w[a].at[side, m_span(h, q)]
+
+    def m_part(a, h, q):
+        if a == 2:
+            return own_w[a].at[m_span(h, q), :]
+        return own_w[a].at[:, m_span(h, q)]
 
     def m_block(a, k):
         if a == 2:
@@ -125,7 +122,7 @@
         return remote(own_w[a], m_block(a, 1), m1_send.at[a], m1_recv.at[a], tx_to(1))
 
     def m_far(a, q):
-        return remote(own_w[a].at[m_span(a, d, q)], m_slot(a, 2, d, q), my_send.at[a, q], my_recv.at[a, q], tx_to(2))
+        return remote(m_part(a, d, q), m_slot(a, 2, d, q), my_send.at[a, q], my_recv.at[a, q], tx_to(2))
 
     def m_swap(a, q):
         return remote(m_slot(a, 2, d, q), m_slot(a, 2, d, q), mx_send.at[a, q], mx_recv.at[a, q], {"dp": 1 - d})
@@ -133,7 +130,7 @@
     def m_pass(a, q, h):
         return remote(m_slot(a, 2, h, q), m_slot(a, 3, h, q), mf_send.at[a, q, h], mf_recv.at[a, q, h], tx_to(1))
 
-    PIECES = [(a, q) for a in range(3) for q in range(2)]
+    PIECES = [(a, q) for q in range(N_PIECES) for a in range(2)] + [(2, q) for q in range(N_PIECES)]
 
     def m_far_start(p):
         m_far(*PIECES[p]).start()
@@ -149,12 +146,13 @@
         m_swap(a, q).wait_recv()
         m_pass(a, q, 1 - d).start()
 
-    def m_ready(a):
+    def m_near_ready(a):
         m_own(a).wait()
         m_near(a).wait_recv()
-        for q in range(2):
-            for h in range(2):
-                m_pass(a, q, h).wait_recv()
+
+    def m_ready(a, q):
+        for h in range(2):
+            m_pass(a, q, h).wait_recv()
 
     def slot(c, dst):
         return pl.ds(aligned((c * n_ty + dst) * ch, ch), ch)
@@ -169,13 +167,18 @@
     def gather(c, src, step):
         return remote(n_buf.at[c, src], n_buf.at[c, src], g_send.at[c, src, (step + 1) // 2], g_recv.at[c, src], {"ty": z + step})
 
-    def reduce(c, dst, step, final):
-        src = work.at[slot(c, dst)]
+    half_full = full // 2
+
+    def cols_of(u):
+        return pl.ds(u * half_full, half_full)
+
+    def reduce(c, u, dst, step, final):
+        src = work.at[slot(c, dst), cols_of(u)]
         if step == 1:
-            return remote(src, landing.at[slot(c, dst)], s_send.at[c, dst], lo_recv.at[c, dst], {"ty": z + 1})
+            return remote(src, landing.at[slot(c, dst), cols_of(u)], s_send.at[c, u, dst], lo_recv.at[c, u, dst], {"ty": z + 1})
         if final:
-            return remote(src, landing2.at[c], s_send.at[c, dst], hi_recv.at[c, 0], {"ty": z - 1})
-        return remote(src, landing.at[slot(c, dst)], s_send.at[c, dst], lo_recv.at[c, dst], {"ty": z - 1})
+            return remote(src, landing2.at[c, :, cols_of(u)], s_send.at[c, u, dst], hi_recv.at[c, u], {"ty": z - 1})
+        return remote(src, landing.at[slot(c, dst), cols_of(u)], s_send.at[c, u, dst], lo_recv.at[c, u, dst], {"ty": z - 1})
 
     def collect(c, k):
         return remote(work.at[slot(c, z), pl.ds(k * width, width)], y_in.at[own_rows(c)], c_send.at[c, k], c_recv.at[c, k], tx_to(k))
@@ -223,6 +226,7 @@
     for k in (2, 3):
         for m in range(3):
             q_copy(k, m, 1 - d).start()
+    m_far_start(0)
     for a in range(3):
         m_own(a).start()
 
@@ -235,34 +239,30 @@
         def _():
             make(-1).start()
 
-    def hop(make, swap, h):
-        @pl.when(z >= h)
-        def _():
-            make(z - h, 1).wait_recv()
-
-            @pl.when(z < last)
-            def _():
-                make(z - h, 1).start()
-
-            if swap is not None:
-                swap(z - h).start()
-
-        @pl.when(z + h <= last)
-        def _():
-            make(z + h, -1).wait_recv()
-
-            @pl.when(z > 0)
-            def _():
-                make(z + h, -1).start()
-
-            if swap is not None:
-                swap(z + h).start()
-
-    def z_hop(g, h):
-        hop(lambda src, step: z_copy(src, g, step), lambda src: zx_copy(src, g), h)
-
-    def p_hop(h):
-        hop(p_copy, px_copy, h)
+    inner = (z > 0) & (z < last)
+
+    def hop(make, swap, h, where):
+        if where != "end":
+            for src, step in ((z - h, 1), (z + h, -1)):
+                @pl.when(inner & (src >= 0) & (src <= last))
+                def _():
+                    make(src, step).wait_recv()
+                    make(src, step).start()
+                    if swap is not None:
+                        swap(src).start()
+        if where != "mid":
+            for src, step, edge in ((z - h, 1, last), (z + h, -1, 0)):
+                @pl.when(z == edge)
+                def _():
+                    make(src, step).wait_recv()
+                    if swap is not None:
+                        swap(src).start()
+
+    def z_hop(g, h, where="both"):
+        hop(lambda src, step: z_copy(src, g, step), lambda src: zx_copy(src, g), h, where)
+
+    def p_hop(h, where):
+        hop(p_copy, px_copy, h, where)
 
     def norm_rows(c):
         block = 32
@@ -279,8 +279,23 @@
 
         lax.fori_loop(0, x_half // block, body, 0)
 
-    s = z // 2
-    order = [z, 1 - z + 4 * s, 2 - s, 3 - 3 * s]
+    def rotary_tables():
+        half_dim = HEAD_DIM // 2
+
+        def body(t, carry):
+            rows = pl.ds(aligned(t * 128, 128), 128)
+            pos = (t * 128 + lax.broadcasted_iota(jnp.int32, (128, HEAD_DIM), 0)).astype(f32)
+            lane = lax.broadcasted_iota(jnp.int32, (128, HEAD_DIM), 1)
+            pair = (lane % half_dim).astype(f32)
+            angles = pos * jnp.exp(pair * (-2.0 / HEAD_DIM * math.log(THETA)))
+            sin_t = jnp.sin(angles)
+            cos_ref[rows, :] = jnp.cos(angles)
+            sin_ref[rows, :] = jnp.where(lane < half_dim, -sin_t, sin_t)
+            return carry
+
+        lax.fori_loop(0, seq_len // 128, body, 0)
+
+    order = [z, (z - 1) * (z - 1) - 2 * (z // 3), 2 + z // 2 - 2 * (z // 3), 3 - 3 * (z // 2)]
 
     def project_heads(src):
         tile = 256
@@ -331,6 +346,7 @@
             q_copy(0, m, h).wait()
         q_copy(1, m, d).wait_recv()
     both_ways(lambda step: z_copy(z, 0, step))
+    rotary_tables()
     for k in (2, 3):
         for m in range(3):
             q_copy(k, m, d).wait_recv()
@@ -348,50 +364,51 @@
     z_hop(0, 2)
     x_copy(1, 2).wait_recv()
     x_copy(1, 3).start()
-    m_far_start(0)
-    m_near(0).start()
+    z_hop(1, 2)
+    both_ways(lambda step: p_copy(z, step))
     x_copy(1, 3).wait_recv()
     norm_rows(1)
-    z_hop(1, 2)
-    both_ways(lambda step: p_copy(z, step))
+    m_near(0).start()
     for m in range(3):
         q_copy(1, m, 1 - d).wait_recv()
-        for k in (2, 3):
+    block_ready(1)
+    project_heads(order[1])
+    attend(order[1])
+    og_start(1)
+    m_far_start(1)
+    z_hop(0, 3)
+    for k in (2, 3):
+        for m in range(3):
             q_copy(k, m, 1 - d).wait_recv()
     project_heads(order[0])
-    z_hop(0, 3)
+    p_hop(1, "mid")
     attend(order[0])
     og_start(0)
-    m_far_start(1)
     m_near(1).start()
+    m_far_start(2)
     z_hop(1, 3)
-    block_ready(1)
-    project_heads(order[1])
-    m_far_done(0)
-    p_hop(1)
-    og_pass(0)
-    attend(order[1])
-    og_start(1)
-    m_far_start(2)
-    p_hop(2)
     block_ready(2)
     project_heads(order[2])
-    m_far_done(1)
-    p_hop(3)
-    og_pass(1)
     attend(order[2])
     og_start(2)
     m_near(2).start()
+    p_hop(2, "mid")
+    og_pass(1)
+    og_pass(0)
+    p_hop(1, "end")
     block_ready(3)
     project_heads(order[3])
-    m_far_done(2)
     attend(order[3])
     og_start(3)
     m_far_start(3)
     m_far_start(4)
+    p_hop(2, "end")
     og_pass(2)
-    m_swap_done(0)
+    p_hop(3, "end")
+    m_far_done(0)
+    m_far_done(1)
     og_pass(3)
+    m_far_done(2)
     for r in range(1, n_ty):
         px_copy(order[r]).wait_recv()
     for r in range(n_ty):
@@ -409,8 +426,11 @@
     for c in range(chunks):
         for k in (2, 3, 1):
             spread(c, k).start()
-    m_far_start(5)
-    m_swap_done(1)
+    for p in range(5, 12):
+        m_far_start(p)
+    for src in range(n_ty):
+        for k in range(1, n_tx):
+            og_copy(src, k).wait_send()
     m_far_done(3)
 
     def norm_chunk(c):
@@ -426,9 +446,16 @@
         both_ways(lambda step: gather(c, z, step))
 
     def gather_hop(c, h):
-        hop(lambda src, step: gather(c, src, step), None, h)
+        hop(lambda src, step: gather(c, src, step), None, h, "mid")
+
+    def gather_ends(c):
+        for h in range(1, n_ty):
+            hop(lambda src, step: gather(c, src, step), None, h, "end")
 
     n_tiles, d_tiles = ff // N_TILE, full // N_TILE
+
+    def chunk_rows(c):
+        return pl.ds(c * n_ty * ch, n_ty * ch)
 
     def gate_up(c, lo, hi):
         def body(t, carry):
@@ -436,106 +463,176 @@
             rows = n_buf[c].reshape(n_ty * ch, full)
             gate_val = jnp.dot(rows, gate_v[:, cols], preferred_element_type=f32).astype(bf16).astype(f32)
             up_val = jnp.dot(rows, up_v[:, cols], preferred_element_type=f32).astype(bf16).astype(f32)
-            act_v[:, cols] = (gate_val * jax.nn.sigmoid(gate_val) * up_val).astype(bf16)
+            o_all[chunk_rows(c), cols] = (gate_val * jax.nn.sigmoid(gate_val) * up_val).astype(bf16)
             return carry
 
         lax.fori_loop(lo, hi, body, 0)
 
-    def down(c, lo, hi):
+    def first_gate_up(q):
+        m_ready(0, q)
+        m_ready(1, q)
+        gate_up(0, q, q + 1)
+        gate_up(0, N_PIECES + q, N_PIECES + q + 1)
+
+    def down(c, u):
         def body(t, carry):
             cols = pl.ds(aligned(t * N_TILE, N_TILE), N_TILE)
-            work[pl.ds(c * n_ty * ch, n_ty * ch), cols] = jnp.dot(act_v[...], down_v[:, cols], preferred_element_type=f32).astype(bf16)
+            work[chunk_rows(c), cols] = jnp.dot(o_all[chunk_rows(c), :], down_v[:, cols], preferred_element_type=f32).astype(bf16)
             return carry
 
-        lax.fori_loop(lo, hi, body, 0)
-
-    def compute(c, third):
-        steps = n_tiles + d_tiles
-        lo, hi = steps * third // 3, steps * (third + 1) // 3
-        if lo < n_tiles:
-            gate_up(c, lo, min(hi, n_tiles))
-        if hi > n_tiles:
-            if c == 0 and lo <= n_tiles:
-                m_swap_done(4)
-                m_swap_done(5)
-                m_ready(2)
-            down(c, max(lo, n_tiles) - n_tiles, hi - n_tiles)
-
-    def add_into(c, dst):
-        work[slot(c, dst), :] = (work[slot(c, dst), :].astype(f32) + landing[slot(c, dst), :].astype(f32)).astype(bf16)
-
-    def reduce_hop(c, h):
+        lax.fori_loop(u * d_tiles // 2, (u + 1) * d_tiles // 2, body, 0)
+
+    def add_into(c, u, dst):
+        rows, cols = slot(c, dst), cols_of(u)
+        work[rows, cols] = (work[rows, cols].astype(f32) + landing[rows, cols].astype(f32)).astype(bf16)
+
+    def reduce_hop(c, u, h):
         dist = n_ty - h
 
         @pl.when(z + dist <= last)
         def _():
             @pl.when(z > 0)
             def _():
-                reduce(c, z + dist, 1, False).wait_recv()
-                add_into(c, z + dist)
-
-            reduce(c, z + dist, 1, False).start()
+                reduce(c, u, z + dist, 1, False).wait_recv()
+                add_into(c, u, z + dist)
+
+            reduce(c, u, z + dist, 1, False).start()
 
         @pl.when(z >= dist)
         def _():
             @pl.when(z < last)
             def _():
-                reduce(c, z - dist, -1, False).wait_recv()
-                add_into(c, z - dist)
-
-            reduce(c, z - dist, -1, dist == 1).start()
-
-    def reduce_end(c):
+                reduce(c, u, z - dist, -1, False).wait_recv()
+                add_into(c, u, z - dist)
+
+            reduce(c, u, z - dist, -1, dist == 1).start()
+
+    def reduce_end(c, u):
+        rows, cols = slot(c, z), cols_of(u)
+
         @pl.when(z > 0)
         def _():
-            reduce(c, z, 1, False).wait_recv()
+            reduce(c, u, z, 1, False).wait_recv()
 
         @pl.when(z < last)
         def _():
-            reduce(c, z, -1, True).wait_recv()
+            reduce(c, u, z, -1, True).wait_recv()
 
         @pl.when(z == 0)
         def _():
-            work[slot(c, z), :] = (work[slot(c, z), :].astype(f32) + landing2[c].astype(f32)).astype(bf16)
+            work[rows, cols] = (work[rows, cols].astype(f32) + landing2[c, :, cols].astype(f32)).astype(bf16)
 
         @pl.when(z == last)
         def _():
-            add_into(c, z)
+            add_into(c, u, z)
 
         @pl.when((z > 0) & (z < last))
         def _():
-            total = work[slot(c, z), :].astype(f32) + landing[slot(c, z), :].astype(f32) + landing2[c].astype(f32)
-            work[slot(c, z), :] = total.astype(bf16)
-
-        for k in (2, 3, 1):
-            collect(c, k).start()
-        y_in[own_rows(c), :] = work[slot(c, z), :width]
-
+            total = work[rows, cols].astype(f32) + landing[rows, cols].astype(f32) + landing2[c, :, cols].astype(f32)
+            work[rows, cols] = total.astype(bf16)
+
+        if u == 0:
+            collect(c, 1).start()
+            y_in[own_rows(c), :] = work[rows, :width]
+        else:
+            collect(c, 2).start()
+            collect(c, 3).start()
+
+    mid = n_tiles // 2
     norm_chunk(0)
     gather_own(0)
-    for c in range(1, chunks):
-        norm_chunk(c)
+    m_far_done(4)
+    norm_chunk(1)
+    m_swap_done(0)
+    norm_chunk(2)
+    m_swap_done(1)
+    norm_chunk(3)
     m_swap_done(2)
-    for t in range(chunks + 2):
-        if 0 < t < chunks:
-            gather_own(t)
-        if t == 1:
-            m_ready(0)
-            m_swap_done(3)
-            m_ready(1)
-        for h in range(1, n_ty):
-            if t >= 2:
-                reduce_hop(t - 2, h)
-            if 1 <= t <= chunks:
-                compute(t - 1, h - 1)
-            if t < chunks:
-                gather_hop(t, h)
-            if t == 0 and h == 1:
-                m_far_done(4)
-            if t == 0 and h == 3:
-                m_far_done(5)
-        if t >= 2:
-            reduce_end(t - 2)
+    gather_hop(0, 1)
+    gather_own(1)
+    m_swap_done(3)
+    for a in range(3):
+        m_near_ready(a)
+    gather_hop(0, 2)
+    m_far_done(5)
+    m_swap_done(4)
+    gather_hop(1, 1)
+    gather_own(2)
+    m_far_done(6)
+    m_swap_done(5)
+    m_far_done(7)
+    gather_hop(1, 2)
+    gather_ends(0)
+    first_gate_up(0)
+    first_gate_up(1)
+    m_swap_done(6)
+    gather_hop(2, 1)
+    gather_own(3)
+    first_gate_up(2)
+    m_swap_done(7)
+    m_far_done(8)
+    first_gate_up(3)
+    down(0, 0)
+    reduce_hop(0, 0, 1)
+    gather_hop(2, 2)
+    m_far_done(9)
+    gather_ends(1)
+    gate_up(1, 0, mid)
+    reduce_hop(0, 0, 2)
+    m_swap_done(8)
+    m_far_done(10)
+    gather_hop(3, 1)
+    gate_up(1, mid, n_tiles)
+    down(1, 0)
+    reduce_hop(1, 0, 1)
+    reduce_hop(0, 0, 3)
+    m_swap_done(9)
+    m_far_done(11)
+    gather_hop(3, 2)
+    gather_ends(2)
+    gate_up(2, 0, mid)
+    reduce_hop(1, 0, 2)
+    m_swap_done(10)
+    reduce_end(0, 0)
+    gate_up(2, mid, n_tiles)
+    reduce_hop(1, 0, 3)
+    m_swap_done(11)
+    for q in range(N_PIECES):
+        m_ready(2, q)
+    down(0, 1)
+    reduce_hop(0, 1, 1)
+    down(2, 0)
+    reduce_hop(2, 0, 1)
+    down(1, 1)
+    reduce_hop(1, 1, 1)
+    reduce_hop(0, 1, 2)
+    down(2, 1)
+    reduce_hop(2, 1, 1)
+    reduce_hop(2, 0, 2)
+    reduce_end(1, 0)
+    gather_ends(3)
+    gate_up(3, 0, mid)
+    reduce_hop(0, 1, 3)
+    reduce_hop(1, 1, 2)
+    reduce_hop(2, 1, 2)
+    gate_up(3, mid, n_tiles)
+    reduce_hop(2, 0, 3)
+    reduce_hop(1, 1, 3)
+    down(3, 0)
+    reduce_hop(3, 0, 1)
+    reduce_end(0, 1)
+    down(3, 1)
+    reduce_hop(3, 1, 1)
+    reduce_hop(2, 1, 3)
+    reduce_end(2, 0)
+    reduce_hop(3, 0, 2)
+    reduce_end(1, 1)
+    reduce_hop(3, 1, 2)
+    reduce_end(2, 1)
+    reduce_hop(3, 0, 3)
+    reduce_hop(3, 1, 3)
+    reduce_end(3, 0)
+    reduce_end(3, 1)
 
     for c in range(chunks):
         for k in range(1, n_tx):
@@ -556,8 +653,6 @@
             q_copy(k, m, d).wait_send()
             q_copy(k, m, 1 - d).wait_send()
     for src in range(n_ty):
-        for k in range(1, n_tx):
-            og_copy(src, k).wait_send()
         for g in range(2):
             @pl.when((z >= src) & (z < last))
             def _():
@@ -571,6 +666,10 @@
             def _():
                 zx_copy(src, g).wait_send()
 
+        @pl.when(z != src)
+        def _():
+            px_copy(src).wait_send()
+
         @pl.when((z >= src) & (z < last))
         def _():
             p_copy(src, 1).wait_send()
@@ -579,12 +678,9 @@
         def _():
             p_copy(src, -1).wait_send()
 
-        @pl.when(z != src)
-        def _():
-            px_copy(src).wait_send()
     for a in range(3):
         m_near(a).wait_send()
-        for q in range(2):
+        for q in range(N_PIECES):
             m_far(a, q).wait_send()
             m_swap(a, q).wait_send()
             for h in range(2):
@@ -602,13 +698,14 @@
             def _():
                 gather(c, src, -1).wait_send()
 
-            @pl.when(z < src)
-            def _():
-                reduce(c, src, 1, False).wait_send()
-
-            @pl.when(z > src)
-            def _():
-                reduce(c, src, -1, False).wait_send()
+            for u in range(2):
+                @pl.when(z < src)
+                def _():
+                    reduce(c, u, src, 1, False).wait_send()
+
+                @pl.when(z > src)
+                def _():
+                    reduce(c, u, src, -1, False).wait_send()
 
 
 def solution(mesh):
@@ -621,13 +718,12 @@
         seq_len, width = x_blk.shape[1:]
         full, ff = N_TX * width, w_gate.shape[1]
         ch = seq_len // N_TX // CHUNKS
-        cos_t, sin_t = rotary_tables(seq_len)
         hbm = pl.BlockSpec(memory_space=pl.ANY)
         vmem = pl.BlockSpec(memory_space=pltpu.VMEM)
         out = pl.pallas_call(
             layer_kernel,
             out_shape=jax.ShapeDtypeStruct((seq_len, width), bf16),
-            in_specs=[hbm] * 8 + [vmem] * 2,
+            in_specs=[hbm] * 8,
             out_specs=vmem,
             scratch_shapes=[
                 pltpu.VMEM((N_TX, seq_len, width), bf16),
@@ -641,27 +737,29 @@
                 pltpu.VMEM((ff, full), bf16),
                 pltpu.VMEM((CHUNKS, ch, full), bf16),
                 pltpu.VMEM((CHUNKS, N_TY, ch, full), bf16),
-                pltpu.VMEM((N_TY * ch, ff), bf16),
                 pltpu.VMEM((seq_len, full), bf16),
                 pltpu.VMEM((seq_len, full), bf16),
                 pltpu.VMEM((CHUNKS, ch, full), bf16),
                 pltpu.VMEM((seq_len, width), bf16),
+                pltpu.VMEM((seq_len, HEAD_DIM), f32),
+                pltpu.VMEM((seq_len, HEAD_DIM), f32),
                 dma((5,)),
                 dma((2, 4)), dma((2, 4)),
                 dma((4, 3, 2)), dma((4, 3, 2)),
                 dma((N_TY, 2, 2)), dma((N_TY, 2)), dma((N_TY, 2)), dma((N_TY, 2)),
                 dma((N_TY, 2)), dma((N_TY,)), dma((N_TY,)), dma((N_TY,)),
                 dma((N_TY, 4)), dma((N_TY, 4)),
-                dma((3,)), dma((3,)), dma((3, 2)), dma((3, 2)), dma((3, 2)), dma((3, 2)), dma((3, 2, 2)), dma((3, 2, 2)),
+                dma((3,)), dma((3,)),
+                dma((3, N_PIECES)), dma((3, N_PIECES)), dma((3, N_PIECES)), dma((3, N_PIECES)), dma((3, N_PIECES, 2)), dma((3, N_PIECES, 2)),
                 dma((CHUNKS, N_TX)), dma((CHUNKS, N_TX)),
                 dma((CHUNKS, N_TY, 2)), dma((CHUNKS, N_TY)),
-                dma((CHUNKS, N_TY)), dma((CHUNKS, N_TY)), dma((CHUNKS, 1)),
+                dma((CHUNKS, 2, N_TY)), dma((CHUNKS, 2, N_TY)), dma((CHUNKS, 2)),
                 dma((CHUNKS, N_TX)), dma((CHUNKS, N_TX)),
             ],
             compiler_params=pltpu.CompilerParams(collective_id=1, has_side_effects=True, vmem_limit_bytes=67043328),
             cost_estimate=pl.CostEstimate(flops=8 * seq_len * full * ff, bytes_accessed=6 * full * ff, transcendentals=seq_len * ff),
             name="layer",
-        )(x_blk[0], w_q, w_k, w_v, w_o, w_gate, w_up, w_down, cos_t, sin_t)
+        )(x_blk[0], w_q, w_k, w_v, w_o, w_gate, w_up, w_down)
         return out[None]
 
     return jax.shard_map(layer_fn, mesh=mesh, in_specs=(act_spec, col_spec, col_spec, col_spec, row_spec, col_spec, col_spec, row_spec), out_specs=act_spec, check_vma=False)

time: 276 us -> 239 us (0.87)
  Pallas kernels: 271 us -> 236 us
  other arithmetic: 3.3 us -> 0 us
    pallas_call x1, Pallas kernels: 271 us -> 236 us  [layer_fn(): pl.pallas_call(layer_kernel, out_shape=jax.ShapeDtypeStruct((seq_len, wid...]
where the time goes in v2:
time: 239 us
  Pallas kernels  236 us (99%)
    pallas_call x1, Pallas kernels, layer_fn(): pl.pallas_call(layer_kernel, out_shape=jax.ShapeDtypeStruct((seq_len, wid...  236 us

profile of v2, /device:TPU:1, one launch (start us, length us, event | category | flops | bytes accessed | tf_op | source)
XLA Modules:
  0.0 238.6 jit_solution(14918363757231720032)
XLA Ops:
  0.0 236.3 %layer.1 = bf16[1024,512]{1,0:T(8,128)(2,1)} custom-call(bf16[1024,512]{1,0:T(8,128)(2,1)} %bitcast.3, bf16[512,512]{1,0:T(8,128)(2,1)} %wq_ref.1, bf16[512,512]{1,0:T(8,128)(2,1)} %wk_ref.1, bf16[512,512]{1,0:T(8,128)(2,1)} %wv_ref.1, bf16[512,512]{1,0:T(8,128)(2,1)} %wo_ref.1, bf16[512,2048]{1,0:T(8,128)(2,1)} %wg_ref.1, bf16[512,2048]{1,0:T(8,128)(2,1)} %wu_ref.1, ...), custom_call_target="tpu_custom_call" | custom-call | flops 34359738368 | bytes 25165824 | tf_op jit(solution)/shard_map/layer/pallas_call | solution.py:723
  236.3 2.3 copy.10

commit v3 on v2

--- a/solution.py
+++ b/solution.py
@@ -26,8 +26,8 @@
     return ((values - mean_val) * lax.rsqrt(var_val + EPS)).astype(bf16)
 
 
-def layer_kernel(x_ref, wq_ref, wk_ref, wv_ref, wo_ref, wg_ref, wu_ref, wd_ref, y_ref,
-                 x_all, w_all, wo_all, qkv_v, o_all, h_v, gate_v, up_v, down_v, h_rows, n_buf, work, landing, landing2, y_in, cos_ref, sin_ref,
+def layer_kernel(x_ref, wq_ref, wk_ref, wv_ref, wo_ref, wg_ref, wu_ref, wd_ref, h_v, y_in,
+                 x_all, w_all, wo_all, qkv_v, o_all, gate_v, up_v, down_v, h_rows, n_buf, work, landing, landing2, cos_ref, sin_ref,
                  loc_sem, x_send, x_recv, q_send, q_recv, z_send, z_recv, zx_send, zx_recv, p_send, p_recv, px_send, px_recv,
                  og_send, og_recv, m1_send, m1_recv, my_send, my_recv, mx_send, mx_recv, mf_send, mf_recv,
                  a_send, a_recv, g_send, g_recv, s_send, lo_recv, hi_recv, c_send, c_recv):
@@ -68,16 +68,16 @@
             return pltpu.make_async_copy(src, dst, q_recv.at[0, m, h])
         return remote(src, dst, q_send.at[k, m, h], q_recv.at[k, m, h], tx_to(k))
 
-    def chip_of(g):
-        return yy if g == 0 else 1 - yy
+    def z_block(src, g):
+        chip = yy if g < 2 else 1 - yy
+        part = core if g % 2 == 0 else 1 - core
+        return w_all.at[src, d, chip, pl.ds(aligned(part * half_w, half_w), half_w)]
 
     def z_copy(src, g, step):
-        block = w_all.at[src, d, chip_of(g)]
-        return remote(block, block, z_send.at[src, g, (step + 1) // 2], z_recv.at[src, g], {"ty": z + step})
+        return remote(z_block(src, g), z_block(src, g), z_send.at[src, g, (step + 1) // 2], z_recv.at[src, g], {"ty": z + step})
 
     def zx_copy(src, g):
-        block = w_all.at[src, d, chip_of(g)]
-        return remote(block, block, zx_send.at[src, g], zx_recv.at[src, g], {"dp": 1 - d})
+        return remote(z_block(src, g), z_block(src, g), zx_send.at[src, g], zx_recv.at[src, g], {"dp": 1 - d})
 
     def p_block(src):
         return wo_all.at[src, pl.ds(aligned(d * half_w, half_w), half_w)]
@@ -85,13 +85,16 @@
     def p_copy(src, step):
         return remote(p_block(src), p_block(src), p_send.at[src, (step + 1) // 2], p_recv.at[src], {"ty": z + step})
 
+    def p_whole(src, step):
+        return remote(wo_all.at[src], wo_all.at[src], p_send.at[src, (step + 1) // 2], p_recv.at[src], {"ty": z + step})
+
     def px_copy(src):
         return remote(p_block(src), p_block(src), px_send.at[src], px_recv.at[src], {"dp": 1 - d})
 
-    def og_copy(src, k):
+    def og_copy(src, k, t):
         head = (i ^ 2) if k == 3 else i
-        block = o_all.at[:, pl.ds(aligned(src * width + head * HEAD_DIM, HEAD_DIM), HEAD_DIM)]
-        return remote(block, block, og_send.at[src, k], og_recv.at[src, k], tx_to(1 if k == 3 else k))
+        block = o_all.at[pl.ds(t * x_half, x_half), pl.ds(aligned(src * width + head * HEAD_DIM, HEAD_DIM), HEAD_DIM)]
+        return remote(block, block, og_send.at[src, k, t], og_recv.at[src, k, t], tx_to(1 if k == 3 else k))
 
     own_w, full_w = (wg_ref, wu_ref, wd_ref), (gate_v, up_v, down_v)
     q_span = ff // 2 // N_PIECES
@@ -223,9 +226,8 @@
         x_copy(c, 1).start()
     for c in range(2):
         x_copy(c, 2).start()
-    for k in (2, 3):
-        for m in range(3):
-            q_copy(k, m, 1 - d).start()
+    for m in range(3):
+        q_copy(2, m, 1 - d).start()
     m_far_start(0)
     for a in range(3):
         m_own(a).start()
@@ -261,8 +263,48 @@
     def z_hop(g, h, where="both"):
         hop(lambda src, step: z_copy(src, g, step), lambda src: zx_copy(src, g), h, where)
 
+    def at_edge(src):
+        return (src == 0) | (src == last)
+
+    def p_step(src, step, onward):
+        @pl.when(at_edge(src))
+        def _():
+            p_whole(src, step).wait_recv()
+            if onward:
+                p_whole(src, step).start()
+
+        @pl.when(jnp.logical_not(at_edge(src)))
+        def _():
+            p_copy(src, step).wait_recv()
+            if onward:
+                p_copy(src, step).start()
+            px_copy(src).start()
+
     def p_hop(h, where):
-        hop(p_copy, px_copy, h, where)
+        if where == "mid":
+            for src, step in ((z - h, 1), (z + h, -1)):
+                @pl.when(inner & (src >= 0) & (src <= last))
+                def _():
+                    p_step(src, step, True)
+        else:
+            for src, step, edge in ((z - h, 1, last), (z + h, -1, 0)):
+                @pl.when(z == edge)
+                def _():
+                    p_step(src, step, False)
+
+    def p_own():
+        @pl.when(z == 0)
+        def _():
+            p_whole(z, 1).start()
+
+        @pl.when(z == last)
+        def _():
+            p_whole(z, -1).start()
+
+        @pl.when(inner)
+        def _():
+            p_copy(z, 1).start()
+            p_copy(z, -1).start()
 
     def norm_rows(c):
         block = 32
@@ -328,44 +370,54 @@
             weights = jnp.exp(scores - jnp.max(scores, axis=-1, keepdims=True))
             probs = (weights * (1.0 / jnp.sum(weights, axis=-1, keepdims=True))).astype(bf16)
             o_all[rows, cols] = jnp.dot(probs, v_all[:keys], preferred_element_type=f32).astype(bf16)
-
-    def og_start(r):
-        og_copy(order[r], 2).start()
-        og_copy(order[r], 1).start()
-
-    def og_pass(r):
-        og_copy(order[r], 2).wait_recv()
-        og_copy(order[r], 3).start()
+            if (blk + 1) * Q_BLOCK % x_half == 0:
+                t = (blk + 1) * Q_BLOCK // x_half - 1
+                og_copy(src, 2, t).start()
+                og_copy(src, 1, t).start()
+
+    def og_pass(r, t):
+        og_copy(order[r], 2, t).wait_recv()
+        og_copy(order[r], 3, t).start()
+
+    def og_ready(r, t):
+        og_copy(order[r], 1, t).wait_recv()
+        og_copy(order[r], 3, t).wait_recv()
 
     def block_ready(r):
-        for g in range(2):
+        for g in range(4):
             zx_copy(order[r], g).wait_recv()
 
     for m in range(3):
-        for h in range(2):
-            q_copy(0, m, h).wait()
-        q_copy(1, m, d).wait_recv()
+        q_copy(0, m, d).wait()
     both_ways(lambda step: z_copy(z, 0, step))
-    rotary_tables()
-    for k in (2, 3):
+    for g in (1, 2, 3):
+        if g == 2:
+            rotary_tables()
+            z_hop(0, 1)
         for m in range(3):
-            q_copy(k, m, d).wait_recv()
-    both_ways(lambda step: z_copy(z, 1, step))
+            q_copy(g, m, d).wait_recv()
+        both_ways(lambda step, g=g: z_copy(z, g, step))
+    zx_copy(z, 3).start()
+    for m in range(3):
+        q_copy(0, m, 1 - d).wait()
     wo_own.wait()
-    z_hop(0, 1)
     x_own.wait()
+    z_hop(1, 1)
     for c in range(2):
         x_copy(c, 1).wait_recv()
     x_copy(0, 2).wait_recv()
     x_copy(0, 3).start()
-    z_hop(1, 1)
+    z_hop(2, 1)
     x_copy(0, 3).wait_recv()
     norm_rows(0)
+    z_hop(3, 1)
     z_hop(0, 2)
+    z_hop(1, 2)
     x_copy(1, 2).wait_recv()
     x_copy(1, 3).start()
-    z_hop(1, 2)
-    both_ways(lambda step: p_copy(z, step))
+    z_hop(2, 2)
+    z_hop(3, 2)
+    p_own()
     x_copy(1, 3).wait_recv()
     norm_rows(1)
     m_near(0).start()
@@ -374,46 +426,44 @@
     block_ready(1)
     project_heads(order[1])
     attend(order[1])
-    og_start(1)
     m_far_start(1)
     z_hop(0, 3)
-    for k in (2, 3):
-        for m in range(3):
-            q_copy(k, m, 1 - d).wait_recv()
+    z_hop(1, 3)
+    for m in range(3):
+        q_copy(2, m, 1 - d).wait_recv()
+    zx_copy(z, 3).wait_recv()
     project_heads(order[0])
     p_hop(1, "mid")
     attend(order[0])
-    og_start(0)
     m_near(1).start()
-    m_far_start(2)
-    z_hop(1, 3)
+    z_hop(2, 3)
+    z_hop(3, 3)
     block_ready(2)
     project_heads(order[2])
     attend(order[2])
-    og_start(2)
     m_near(2).start()
     p_hop(2, "mid")
-    og_pass(1)
-    og_pass(0)
     p_hop(1, "end")
     block_ready(3)
     project_heads(order[3])
     attend(order[3])
-    og_start(3)
-    m_far_start(3)
-    m_far_start(4)
+    m_far_start(2)
     p_hop(2, "end")
-    og_pass(2)
-    p_hop(3, "end")
+    for r in (1, 0, 2):
+        for t in range(2):
+            og_pass(r, t)
+    og_pass(3, 0)
+    og_pass(3, 1)
     m_far_done(0)
     m_far_done(1)
-    og_pass(3)
-    m_far_done(2)
-    for r in range(1, n_ty):
-        px_copy(order[r]).wait_recv()
-    for r in range(n_ty):
-        og_copy(order[r], 1).wait_recv()
-        og_copy(order[r], 3).wait_recv()
+    p_hop(3, "end")
+    for r in range(3):
+        for t in range(2):
+            og_ready(r, t)
+    for src in range(1, last):
+        @pl.when(z != src)
+        def _():
+            px_copy(src).wait_recv()
 
     def out_project(t, carry):
         rows = pl.ds(aligned(t * 256, 256), 256)
@@ -421,17 +471,20 @@
         h_v[rows, :] = (x_all[i, rows, :].astype(f32) + attn_out.astype(f32)).astype(bf16)
         return carry
 
-    lax.fori_loop(0, seq_len // 256, out_project, 0)
-
-    for c in range(chunks):
+    og_ready(3, 0)
+    lax.fori_loop(0, seq_len // 512, out_project, 0)
+    og_ready(3, 1)
+    lax.fori_loop(seq_len // 512, seq_len // 256, out_project, 0)
+
+    for c, pieces in ((0, ()), (1, (3,)), (2, (4, 5)), (3, (6, 7, 8, 9, 10, 11))):
         for k in (2, 3, 1):
             spread(c, k).start()
-    for p in range(5, 12):
-        m_far_start(p)
+        for p in pieces:
+            m_far_start(p)
     for src in range(n_ty):
         for k in range(1, n_tx):
-            og_copy(src, k).wait_send()
-    m_far_done(3)
+            for t in range(2):
+                og_copy(src, k, t).wait_send()
 
     def norm_chunk(c):
         for k in range(1, n_tx):
@@ -541,109 +594,104 @@
     mid = n_tiles // 2
     norm_chunk(0)
     gather_own(0)
-    m_far_done(4)
+    m_swap_done(0)
+    m_far_done(2)
+    m_swap_done(1)
     norm_chunk(1)
-    m_swap_done(0)
-    norm_chunk(2)
-    m_swap_done(1)
-    norm_chunk(3)
-    m_swap_done(2)
+    for a in range(3):
+        m_near_ready(a)
     gather_hop(0, 1)
     gather_own(1)
-    m_swap_done(3)
-    for a in range(3):
-        m_near_ready(a)
+    m_swap_done(2)
+    m_far_done(3)
+    norm_chunk(2)
     gather_hop(0, 2)
-    m_far_done(5)
-    m_swap_done(4)
+    m_far_done(4)
     gather_hop(1, 1)
     gather_own(2)
-    m_far_done(6)
-    m_swap_done(5)
-    m_far_done(7)
+    m_swap_done(3)
+    m_far_done(5)
     gather_hop(1, 2)
     gather_ends(0)
     first_gate_up(0)
+    m_swap_done(4)
     first_gate_up(1)
-    m_swap_done(6)
+    norm_chunk(3)
+    m_far_done(6)
     gather_hop(2, 1)
     gather_own(3)
+    m_swap_done(5)
     first_gate_up(2)
+    m_far_done(7)
+    m_swap_done(6)
     m_swap_done(7)
     m_far_done(8)
     first_gate_up(3)
     down(0, 0)
     reduce_hop(0, 0, 1)
+    m_far_done(9)
     gather_hop(2, 2)
-    m_far_done(9)
     gather_ends(1)
     gate_up(1, 0, mid)
+    gather_hop(3, 1)
     reduce_hop(0, 0, 2)
-    m_swap_done(8)
+    gate_up(1, mid, n_tiles)
     m_far_done(10)
-    gather_hop(3, 1)
-    gate_up(1, mid, n_tiles)
     down(1, 0)
     reduce_hop(1, 0, 1)
     reduce_hop(0, 0, 3)
-    m_swap_done(9)
+    gather_hop(3, 2)
+    m_swap_done(8)
     m_far_done(11)
-    gather_hop(3, 2)
+    reduce_hop(1, 0, 2)
     gather_ends(2)
     gate_up(2, 0, mid)
-    reduce_hop(1, 0, 2)
+    m_swap_done(9)
+    reduce_hop(1, 0, 3)
     m_swap_done(10)
-    reduce_end(0, 0)
     gate_up(2, mid, n_tiles)
-    reduce_hop(1, 0, 3)
+    down(2, 0)
+    reduce_hop(2, 0, 1)
     m_swap_done(11)
     for q in range(N_PIECES):
         m_ready(2, q)
     down(0, 1)
     reduce_hop(0, 1, 1)
-    down(2, 0)
-    reduce_hop(2, 0, 1)
+    reduce_end(0, 0)
     down(1, 1)
     reduce_hop(1, 1, 1)
     reduce_hop(0, 1, 2)
+    reduce_hop(1, 1, 2)
     down(2, 1)
     reduce_hop(2, 1, 1)
-    reduce_hop(2, 0, 2)
     reduce_end(1, 0)
+    reduce_hop(0, 1, 3)
     gather_ends(3)
     gate_up(3, 0, mid)
-    reduce_hop(0, 1, 3)
-    reduce_hop(1, 1, 2)
+    reduce_hop(1, 1, 3)
+    reduce_hop(2, 0, 2)
     reduce_hop(2, 1, 2)
     gate_up(3, mid, n_tiles)
     reduce_hop(2, 0, 3)
-    reduce_hop(1, 1, 3)
+    down(3, 1)
+    reduce_hop(3, 1, 1)
+    reduce_end(0, 1)
     down(3, 0)
     reduce_hop(3, 0, 1)
-    reduce_end(0, 1)
-    down(3, 1)
-    reduce_hop(3, 1, 1)
     reduce_hop(2, 1, 3)
+    reduce_end(1, 1)
     reduce_end(2, 0)
+    reduce_hop(3, 1, 2)
     reduce_hop(3, 0, 2)
-    reduce_end(1, 1)
-    reduce_hop(3, 1, 2)
     reduce_end(2, 1)
+    reduce_hop(3, 1, 3)
     reduce_hop(3, 0, 3)
-    reduce_hop(3, 1, 3)
+    reduce_end(3, 1)
     reduce_end(3, 0)
-    reduce_end(3, 1)
 
     for c in range(chunks):
         for k in range(1, n_tx):
             collect(c, k).wait_recv()
-
-    def finish(t, carry):
-        rows = pl.ds(aligned(t * 128, 128), 128)
-        y_ref[rows, :] = (h_v[rows, :].astype(f32) + y_in[rows, :].astype(f32)).astype(bf16)
-        return carry
-
-    lax.fori_loop(0, seq_len // 128, finish, 0)
 
     for c in range(2):
         for k in range(1, n_tx):
@@ -651,9 +699,10 @@
     for k in range(1, n_tx):
         for m in range(3):
             q_copy(k, m, d).wait_send()
-            q_copy(k, m, 1 - d).wait_send()
+            if k < 3:
+                q_copy(k, m, 1 - d).wait_send()
     for src in range(n_ty):
-        for g in range(2):
+        for g in range(4):
             @pl.when((z >= src) & (z < last))
             def _():
                 z_copy(src, g, 1).wait_send()
@@ -662,21 +711,28 @@
             def _():
                 z_copy(src, g, -1).wait_send()
 
+            if g == 3:
+                zx_copy(src, g).wait_send()
+            else:
+                @pl.when(z != src)
+                def _():
+                    zx_copy(src, g).wait_send()
+
+        inner_src = 0 < src < last
+        if inner_src:
             @pl.when(z != src)
             def _():
-                zx_copy(src, g).wait_send()
-
-        @pl.when(z != src)
-        def _():
-            px_copy(src).wait_send()
+                px_copy(src).wait_send()
+
+        p_any = p_copy if inner_src else p_whole
 
         @pl.when((z >= src) & (z < last))
         def _():
-            p_copy(src, 1).wait_send()
+            p_any(src, 1).wait_send()
 
         @pl.when((z <= src) & (z > 0))
         def _():
-            p_copy(src, -1).wait_send()
+            p_any(src, -1).wait_send()
 
     for a in range(3):
         m_near(a).wait_send()
@@ -720,18 +776,17 @@
         ch = seq_len // N_TX // CHUNKS
         hbm = pl.BlockSpec(memory_space=pl.ANY)
         vmem = pl.BlockSpec(memory_space=pltpu.VMEM)
-        out = pl.pallas_call(
+        resid_h, mlp_out = pl.pallas_call(
             layer_kernel,
-            out_shape=jax.ShapeDtypeStruct((seq_len, width), bf16),
+            out_shape=[jax.ShapeDtypeStruct((seq_len, width), bf16)] * 2,
             in_specs=[hbm] * 8,
-            out_specs=vmem,
+            out_specs=[vmem] * 2,
             scratch_shapes=[
                 pltpu.VMEM((N_TX, seq_len, width), bf16),
                 pltpu.VMEM((N_TY, 2, 2, width, 3 * HEAD_DIM), bf16),
                 pltpu.VMEM((N_TY, width, width), bf16),
                 pltpu.VMEM((seq_len, 3 * HEAD_DIM), bf16),
                 pltpu.VMEM((seq_len, full), bf16),
-                pltpu.VMEM((seq_len, width), bf16),
                 pltpu.VMEM((full, ff), bf16),
                 pltpu.VMEM((full, ff), bf16),
                 pltpu.VMEM((ff, full), bf16),
@@ -740,15 +795,14 @@
                 pltpu.VMEM((seq_len, full), bf16),
                 pltpu.VMEM((seq_len, full), bf16),
                 pltpu.VMEM((CHUNKS, ch, full), bf16),
-                pltpu.VMEM((seq_len, width), bf16),
                 pltpu.VMEM((seq_len, HEAD_DIM), f32),
                 pltpu.VMEM((seq_len, HEAD_DIM), f32),
                 dma((5,)),
                 dma((2, 4)), dma((2, 4)),
                 dma((4, 3, 2)), dma((4, 3, 2)),
-                dma((N_TY, 2, 2)), dma((N_TY, 2)), dma((N_TY, 2)), dma((N_TY, 2)),
+                dma((N_TY, 4, 2)), dma((N_TY, 4)), dma((N_TY, 4)), dma((N_TY, 4)),
                 dma((N_TY, 2)), dma((N_TY,)), dma((N_TY,)), dma((N_TY,)),
-                dma((N_TY, 4)), dma((N_TY, 4)),
+                dma((N_TY, 4, 2)), dma((N_TY, 4, 2)),
                 dma((3,)), dma((3,)),
                 dma((3, N_PIECES)), dma((3, N_PIECES)), dma((3, N_PIECES)), dma((3, N_PIECES)), dma((3, N_PIECES, 2)), dma((3, N_PIECES, 2)),
                 dma((CHUNKS, N_TX)), dma((CHUNKS, N_TX)),
@@ -756,10 +810,10 @@
                 dma((CHUNKS, 2, N_TY)), dma((CHUNKS, 2, N_TY)), dma((CHUNKS, 2)),
                 dma((CHUNKS, N_TX)), dma((CHUNKS, N_TX)),
             ],
-            compiler_params=pltpu.CompilerParams(collective_id=1, has_side_effects=True, vmem_limit_bytes=67043328),
+            compiler_params=pltpu.CompilerParams(collective_id=1, has_side_effects=True, vmem_limit_bytes=64487424),
             cost_estimate=pl.CostEstimate(flops=8 * seq_len * full * ff, bytes_accessed=6 * full * ff, transcendentals=seq_len * ff),
             name="layer",
         )(x_blk[0], w_q, w_k, w_v, w_o, w_gate, w_up, w_down)
-        return out[None]
+        return (resid_h.astype(f32) + mlp_out.astype(f32)).astype(bf16)[None]
 
     return jax.shard_map(layer_fn, mesh=mesh, in_specs=(act_spec, col_spec, col_spec, col_spec, row_spec, col_spec, col_spec, row_spec), out_specs=act_spec, check_vma=False)

time: 239 us -> 221 us (0.925)
  Pallas kernels: 236 us -> 217 us
  other arithmetic: 0 us -> 2.8 us
    pallas_call x1, Pallas kernels: 236 us -> 217 us  [layer_fn(): pl.pallas_call(layer_kernel, out_shape=[jax.ShapeDtypeStruct((seq_len, wi...]
    broadcast_in_dim x0 -> x1, other arithmetic: none -> 2.8 us  [layer_fn(): return (resid_h.astype(f32) + mlp_out.astype(f32)).astype(bf16)[None]]
where the time goes in v3:
time: 221 us; the launch traced here: 220 us
  Pallas kernels  217 us (98%)
  other arithmetic  2.8 us (1%)
    pallas_call x1, Pallas kernels, layer_fn(): pl.pallas_call(layer_kernel, out_shape=[jax.ShapeDtypeStruct((seq_len, wi...  217 us

profile of v3, /device:TPU:1, one launch (start us, length us, event | category | flops | bytes accessed | tf_op | source)
XLA Modules:
  0.0 219.8 jit_solution(13543441926881658241)
XLA Ops:
  0.0 217.0 %layer.1 = (bf16[1024,512]{1,0:T(8,128)(2,1)}, bf16[1024,512]{1,0:T(8,128)(2,1)}) custom-call(bf16[1024,512]{1,0:T(8,128)(2,1)} %bitcast.3, bf16[512,512]{1,0:T(8,128)(2,1)} %wq_ref.1, bf16[512,512]{1,0:T(8,128)(2,1)} %wk_ref.1, bf16[512,512]{1,0:T(8,128)(2,1)} %wv_ref.1, bf16[512,512]{1,0:T(8,128)(2,1)} %wo_ref.1, bf16[512,2048]{1,0:T(8,128)(2,1)} %wg_ref.1, ...), custom_call_target="tpu_custom_call" | custom-call | flops 34359738368 | bytes 25165824 | tf_op jit(solution)/shard_map/layer/pallas_call | solution.py:779
  217.0 2.8 %fusion = bf16[1,1024,512]{2,1,0:T(8,128)(2,1)} fusion(bf16[1024,512]{1,0:T(8,128)(2,1)} %get-tuple-element.8, bf16[1024,512]{1,0:T(8,128)(2,1)} %get-tuple-element.7), kind=kLoop, calls=%fused_computation.1 | loop fusion | flops 2097152 | bytes 3145728 | tf_op jit(solution)/shard_map/broadcast_in_dim | solution.py:817
